TPU v7x, 32 devices: a 4x4x1 block of a 4x4x8 slice. The times are simulated.
32 devices in a mesh: replica: 1 (over z), data: 4 (over y), table: 8 (over x, core).
Axes of the slice: x: 4, y: 4, z: 1, core: 2. Of those that a mesh axis runs over, the one named last changes fastest.
The devices are a block of a 4x4x8 slice.
Arguments:
- tokens: bfloat16 [4096, 1024], P(('replica', 'data', 'table'))
- grad_out: bfloat16 [4096, 1024], P(('replica', 'data', 'table'))
- table_u: bfloat16 [131072, 1024], P(('replica', 'table'))
- table_v: bfloat16 [131072, 1024], P(('replica', 'table'))
- wanted_ids: int32 [32, 256], P(('replica', 'data', 'table'))
- pick_idx: int32 [4096, 4, 32], P(('replica', 'data', 'table'))
- gate_val: float32 [4096, 4, 32], P(('replica', 'data', 'table'))
Outputs:
- output 1: bfloat16 [4096, 1024], P(('replica', 'data', 'table'))
- output 2: bfloat16 [4096, 1024], P(('replica', 'data', 'table'))
- output 3: bfloat16 [131072, 1024], P(('replica', 'table'))
- output 4: bfloat16 [131072, 1024], P(('replica', 'table'))
All inputs are finite; a program needn't handle non-finite values.
Results may differ from a plain program's by a relative error of at most 0.00775731.
Values are sent between devices in bfloat16 or wider.
A program may use at most 768 MiB of HBM per device.

v0:
```python
import math
import jax
import jax.numpy as jnp
from jax import lax
from jax.sharding import PartitionSpec as P, NamedSharding


def gelu_pair(pre_act):
    cdf_val = 0.5 * (1.0 + lax.erf(pre_act * 0.7071067811865476))
    pdf_val = jnp.exp(-0.5 * pre_act * pre_act) * 0.3989422804014327
    return pre_act * cdf_val, cdf_val + pre_act * pdf_val


def token_pass(tok_loc, dy_loc, rows_u, rows_v, pick_loc, gate_loc):
    tok_local, width = tok_loc.shape
    sel_tok = pick_loc.shape[1] * pick_loc.shape[2]
    block_len = math.gcd(tok_local, max(1, 8192 // sel_tok))
    num_blocks = tok_local // block_len
    inputs = (tok_loc.reshape(num_blocks, block_len, width), dy_loc.reshape(num_blocks, block_len, width), pick_loc.reshape(num_blocks, block_len, sel_tok), gate_loc.reshape(num_blocks, block_len, sel_tok))

    def body(acc_pair, block_in):
        acc_u, acc_v = acc_pair
        x_blk, dy_blk, pick_blk, gate_blk = block_in
        sel_u = jnp.take(rows_u, pick_blk, axis=0, mode='clip')
        sel_v = jnp.take(rows_v, pick_blk, axis=0, mode='clip')
        pre_act = jnp.einsum('bsd,bd->bs', sel_u, x_blk, preferred_element_type=jnp.float32)
        act_val, slope_val = gelu_pair(pre_act)
        weight = gate_blk * act_val
        y_blk = jnp.einsum('bs,bsd->bd', weight, sel_v, preferred_element_type=jnp.float32)
        v_dot_dy = jnp.einsum('bsd,bd->bs', sel_v, dy_blk, preferred_element_type=jnp.float32)
        coef_sel = gate_blk * slope_val * v_dot_dy
        dx_blk = jnp.einsum('bs,bsd->bd', coef_sel, sel_u, preferred_element_type=jnp.float32)
        flat_pick = pick_blk.reshape(-1)
        acc_u = acc_u.at[flat_pick].add((coef_sel[:, :, None] * x_blk[:, None, :]).reshape(-1, width))
        acc_v = acc_v.at[flat_pick].add((weight[:, :, None] * dy_blk[:, None, :]).reshape(-1, width))
        return (acc_u, acc_v), (y_blk.astype(jnp.bfloat16), dx_blk.astype(jnp.bfloat16))

    zero_acc = jnp.zeros((rows_u.shape[0], width), jnp.float32)
    (acc_u, acc_v), (y_st, dx_st) = lax.scan(body, (zero_acc, zero_acc), inputs)
    return y_st.reshape(tok_local, width), dx_st.reshape(tok_local, width), acc_u, acc_v


def solution(mesh):
    table_n = mesh.shape['table']
    tok_spec = P(('replica', 'data', 'table'))
    row_spec = P(('replica', 'table'))

    def device_step(tok_loc, dy_loc, u_loc, v_loc, wanted_loc, pick_loc, gate_loc):
        n_local, width = u_loc.shape
        pool_len = wanted_loc.shape[1] // table_n
        owner_base = jnp.arange(table_n, dtype=jnp.int32)[:, None] * n_local
        requests = wanted_loc.reshape(table_n, pool_len) - owner_base
        asked_rows = lax.all_to_all(requests, 'table', 0, 0, tiled=True)
        sent_u = jnp.take(u_loc, asked_rows, axis=0, mode='clip')
        sent_v = jnp.take(v_loc, asked_rows, axis=0, mode='clip')
        rows_u = lax.all_to_all(sent_u, 'table', 0, 0, tiled=True).reshape(table_n * pool_len, width)
        rows_v = lax.all_to_all(sent_v, 'table', 0, 0, tiled=True).reshape(table_n * pool_len, width)
        y_loc, dx_loc, part_u, part_v = token_pass(tok_loc, dy_loc, rows_u, rows_v, pick_loc, gate_loc)
        back_u = lax.all_to_all(part_u.astype(jnp.bfloat16).reshape(table_n, pool_len, width), 'table', 0, 0, tiled=True)
        back_v = lax.all_to_all(part_v.astype(jnp.bfloat16).reshape(table_n, pool_len, width), 'table', 0, 0, tiled=True)
        flat_rows = asked_rows.reshape(-1)
        grad_u = jnp.zeros((n_local, width), jnp.float32).at[flat_rows].add(back_u.reshape(-1, width).astype(jnp.float32))
        grad_v = jnp.zeros((n_local, width), jnp.float32).at[flat_rows].add(back_v.reshape(-1, width).astype(jnp.float32))
        grad_u = lax.psum(grad_u, 'data')
        grad_v = lax.psum(grad_v, 'data')
        return y_loc, dx_loc, grad_u.astype(jnp.bfloat16), grad_v.astype(jnp.bfloat16)

    return jax.shard_map(device_step, mesh=mesh, in_specs=(tok_spec, tok_spec, row_spec, row_spec, tok_spec, tok_spec, tok_spec), out_specs=(tok_spec, tok_spec, row_spec, row_spec), check_vma=False)
```

profile of v0, /device:TPU:97, one launch (start us, length us, event | category | flops | bytes accessed | tf_op | source)
XLA Modules:
  0.0 2980.6 jit_solution(4269951728581618843)
XLA Ops:
  0.6 0.5 broadcast.136
  1.2 1.3 reduce.8
  2.5 0.1 reshape.176
  2.7 10.4 all_to_all.26
  13.1 0.7 reduce.9
  13.8 0.1 reshape.206
  13.9 4.0 gather_fusion.3
  17.9 4.7 all-to-all-start.2
  22.6 4.0 gather_fusion.2
  26.6 5.3 all-to-all-done.2
  31.9 5.1 all-to-all-start.1
  37.0 1.0 reshape.174
  38.0 0.7 copy.15
  38.7 1.0 reshape.175
  39.7 0.7 copy.16
  40.4 6.0 all-to-all-done.1
  46.4 1.1 broadcast_in_dim.29.clone
  47.5 1.1 broadcast_in_dim.29
  48.6 566.6 %while.16 = (s32[]{:T(128)}, f32[256,1024]{1,0:T(8,128)}, f32[256,1024]{1,0:T(8,128)}, bf16[2,64,1024]{2,1,0:T(8,128)(2,1)}, bf16[2,64,1024]{2,1,0:T(8,128)(2,1)...) while((s32[]{:T(128)}, f32[256,1024]{1,0:T(8,128)}, ...), condition=%wide.region_3.4_spmd, body=%wide.region_0.3_spmd.sunk | while | flops 100925440 | bytes 465961344 | solution.py:39
  48.6 0.8 bitcast_clamp_fusion.2
  49.4 0.9 bitcast_convert_fusion.7
  50.4 1.6 dynamic-slice_bitcast_fusion.3
  52.0 41.6 %gather_fusion.1 = bf16[8192,1024]{1,0:T(8,128)(2,1)} fusion(bf16[256,1024]{1,0:T(8,128)(2,1)} %get-tuple-element.244, s32[8192]{0:T(1024)S(1)} %get-tuple-element.203), kind=kCustom, calls=%fused_computation.1.clone.1 | custom fusion | bytes 33587200 | tf_op jit(solution)/shard_map/while/body/eval_jaxpr/jit(_take)/gather | solution.py:25
  93.6 8.0 fusion.44
  101.6 41.6 %gather_fusion = bf16[8192,1024]{1,0:T(8,128)(2,1)} fusion(bf16[256,1024]{1,0:T(8,128)(2,1)} %get-tuple-element.242, s32[8192]{0:T(1024)S(1)} %get-tuple-element.203), kind=kCustom, calls=%fused_computation.clone.1 | custom fusion | bytes 33587200 | tf_op jit(solution)/shard_map/while/body/eval_jaxpr/jit(_take)/gather | solution.py:24
  143.2 8.2 fusion.43
  151.4 1.0 bitcast_multiply_fusion.6
  152.5 8.2 fusion.46
  160.7 2.3 fusion.45
  163.0 0.8 fusion.47
  163.8 11.3 bitcast_multiply_fusion.8
  175.1 73.2 %scatter_fusion.1 = f32[256,1024]{1,0:T(8,128)} fusion(f32[256,1024]{1,0:T(8,128)} %get-tuple-element.225, s32[8192]{0:T(1024)S(1)} %bitcast.139, f32[8192,1024]{1,0:T(8,128)} %bitcast_multiply_fusion.8), kind=kCustom, calls=%fused_computation.5.clone.1 | custom fusion | flops 8388608 | bytes 100696064 | tf_op jit(solution)/shard_map/while/body/eval_jaxpr/scatter-add | solution.py:35
  248.3 11.3 bitcast_multiply_fusion.7
  259.6 71.3 %scatter_fusion = f32[256,1024]{1,0:T(8,128)S(1)} fusion(f32[256,1024]{1,0:T(8,128)S(1)} %copy-done, s32[8192]{0:T(1024)S(1)} %bitcast.140, f32[8192,1024]{1,0:T(8,128)} %bitcast_multiply_fusion.7), kind=kCustom, calls=%fused_computation.4.clone.1 | custom fusion | flops 8388608 | bytes 100696064 | tf_op jit(solution)/shard_map/while/body/eval_jaxpr/scatter-add | solution.py:34
  331.0 1.0 copy-done.1
  331.9 0.8 bitcast_clamp_fusion.2
  332.7 0.9 bitcast_convert_fusion.7
  333.7 1.6 dynamic-slice_bitcast_fusion.3
  335.3 41.6 %gather_fusion.1 = bf16[8192,1024]{1,0:T(8,128)(2,1)} fusion(bf16[256,1024]{1,0:T(8,128)(2,1)} %get-tuple-element.244, s32[8192]{0:T(1024)S(1)} %get-tuple-element.203), kind=kCustom, calls=%fused_computation.1.clone.1 | custom fusion | bytes 33587200 | tf_op jit(solution)/shard_map/while/body/eval_jaxpr/jit(_take)/gather | solution.py:25
  376.9 8.0 fusion.44
  384.9 41.6 %gather_fusion = bf16[8192,1024]{1,0:T(8,128)(2,1)} fusion(bf16[256,1024]{1,0:T(8,128)(2,1)} %get-tuple-element.242, s32[8192]{0:T(1024)S(1)} %get-tuple-element.203), kind=kCustom, calls=%fused_computation.clone.1 | custom fusion | bytes 33587200 | tf_op jit(solution)/shard_map/while/body/eval_jaxpr/jit(_take)/gather | solution.py:24
  426.5 8.2 fusion.43
  434.7 1.0 bitcast_multiply_fusion.6
  435.7 8.2 fusion.46
  444.0 2.3 fusion.45
  446.3 0.8 fusion.47
  447.1 11.3 bitcast_multiply_fusion.8
  458.4 73.2 %scatter_fusion.1 = f32[256,1024]{1,0:T(8,128)} fusion(f32[256,1024]{1,0:T(8,128)} %get-tuple-element.225, s32[8192]{0:T(1024)S(1)} %bitcast.139, f32[8192,1024]{1,0:T(8,128)} %bitcast_multiply_fusion.8), kind=kCustom, calls=%fused_computation.5.clone.1 | custom fusion | flops 8388608 | bytes 100696064 | tf_op jit(solution)/shard_map/while/body/eval_jaxpr/scatter-add | solution.py:35
  531.5 11.3 bitcast_multiply_fusion.7
  542.9 71.3 %scatter_fusion = f32[256,1024]{1,0:T(8,128)S(1)} fusion(f32[256,1024]{1,0:T(8,128)S(1)} %copy-done, s32[8192]{0:T(1024)S(1)} %bitcast.140, f32[8192,1024]{1,0:T(8,128)} %bitcast_multiply_fusion.7), kind=kCustom, calls=%fused_computation.4.clone.1 | custom fusion | flops 8388608 | bytes 100696064 | tf_op jit(solution)/shard_map/while/body/eval_jaxpr/scatter-add | solution.py:34
  614.3 1.0 copy-done.1
  615.2 2.1 convert_element_type.46
  617.3 4.5 all-to-all-start.3
  621.8 0.1 reshape.183
  621.9 2.1 convert_element_type.50
  624.0 7.1 all-to-all-done.3
  631.0 4.6 all-to-all-start.4
  635.6 0.1 bitcast_convert_fusion.5
  635.8 21.3 broadcast.91.clone
  657.0 35.2 %scatter_fusion.2 = f32[16384,1024]{1,0:T(8,128)} fusion(f32[16384,1024]{1,0:T(8,128)} %broadcast.91.clone, s32[256]{0:T(256)S(1)} %bitcast.147, f32[256,1024]{1,0:T(8,128)S(1)} %bitcast_convert_fusion.5), kind=kCustom, calls=%fused_computation.6 | custom fusion | flops 262144 | bytes 3146752 | tf_op jit(solution)/shard_map/scatter-add | solution.py:62
  692.2 0.1 bitcast_convert_fusion.4
  692.4 21.3 broadcast.91.clone.1
  713.6 35.2 %scatter_fusion.3 = f32[16384,1024]{1,0:T(8,128)} fusion(f32[16384,1024]{1,0:T(8,128)} %broadcast.91.clone.1, s32[256]{0:T(256)S(1)} %bitcast.148, f32[256,1024]{1,0:T(8,128)S(1)} %bitcast_convert_fusion.4), kind=kCustom, calls=%fused_computation.7 | custom fusion | flops 262144 | bytes 3146752 | tf_op jit(solution)/shard_map/scatter-add | solution.py:63
  748.9 2231.7 %all-reduce.2 = (bf16[16384,1024]{1,0:T(8,128)(2,1)}, bf16[16384,1024]{1,0:T(8,128)(2,1)}) all-reduce(f32[16384,1024]{1,0:T(8,128)} %scatter_fusion.2, f32[16384,1024]{1,0:T(8,128)} %scatter_fusion.3), channel_id=1, replica_groups=mesh['replica'=1,'data'=4,'table'=8] {'data'}, use_global_device_ids=true, to_apply=%region_5.6 | all-reduce | flops 33554432 | bytes 201326592 | tf_op jit(solution)/shard_map/psum | solution.py:64
  (49 shorter events, 0.2 us)
Async XLA Ops:
  13.1 24.0 copy-start.5
  17.9 14.1 all-to-all-start.2
  31.9 14.4 all-to-all-start.1
  48.6 573.2 %copy-start.6 = (s32[8,1,32]{2,1,0:T(1,128)S(1)}, s32[8,1,32]{2,1,0:T(1,128)}, u32[]{:S(2)}) copy-start(s32[8,1,32]{2,1,0:T(1,128)} %copy-done.5) | copy-start | bytes 3076
  143.2 17.4 slice-start
  143.2 17.4 slice-start.1
  143.2 17.4 slice-start.2
  152.4 11.3 copy-start.3
  152.4 8.2 slice-start.3
  175.1 73.2 %copy-start.2 = (f32[64,1024]{1,0:T(8,128)S(1)}, f32[64,1024]{1,0:T(8,128)}, u32[]{:S(2)}) copy-start(f32[64,1024]{1,0:T(8,128)} %get-tuple-element.202) | copy-start | bytes 786436 | tf_op jit(solution)/shard_map/while
  175.1 73.2 %copy-start.4 = (f32[64,128]{1,0:T(8,128)S(1)}, f32[64,128]{1,0:T(8,128)}, u32[]{:S(2)}) copy-start(f32[64,128]{1,0:T(8,128)} %copy-done.3) | copy-start | bytes 98308 | tf_op jit(solution)/shard_map/while
  248.3 11.3 copy-start
  331.0 1.0 copy-start.1
  426.5 17.4 slice-start
  426.5 17.4 slice-start.1
  426.5 17.4 slice-start.2
  435.7 11.3 copy-start.3
  435.7 8.2 slice-start.3
  458.4 73.2 %copy-start.2 = (f32[64,1024]{1,0:T(8,128)S(1)}, f32[64,1024]{1,0:T(8,128)}, u32[]{:S(2)}) copy-start(f32[64,1024]{1,0:T(8,128)} %get-tuple-element.202) | copy-start | bytes 786436 | tf_op jit(solution)/shard_map/while
  458.4 73.2 %copy-start.4 = (f32[64,128]{1,0:T(8,128)S(1)}, f32[64,128]{1,0:T(8,128)}, u32[]{:S(2)}) copy-start(f32[64,128]{1,0:T(8,128)} %copy-done.3) | copy-start | bytes 98308 | tf_op jit(solution)/shard_map/while
  531.5 11.3 copy-start
  614.2 1.0 copy-start.1
  617.3 13.7 all-to-all-start.3
  631.0 61.2 %all-to-all-start.4 = ((bf16[8,32,1024]{2,1,0:T(8,128)(2,1)}), bf16[8,32,1024]{2,1,0:T(8,128)(2,1)S(1)}, u32[]{:S(2)}, u32[]{:S(2)}) async-start(bf16[8,32,1024]{2,1,0:T(8,128)(2,1)} %bitcast.37), calls=%async_computation.4 | async-start | bytes 1048576 | tf_op jit(solution)/shard_map/all_to_all | solution.py:60
where the time goes:
time: 2990 us; the launch traced here: 2980 us
  blocking collectives  2240 us (75%)
  other arithmetic  420 us (14%)
  local copies, waits for them, and re-layouts  227 us (8%)
  matrix products  53.4 us (2%)
    psum x1, blocking collectives, device_step(): grad_u = lax.psum(grad_u, 'data')  2230 us
    scatter-add x2, other arithmetic, body(): acc_v.at[flat_pick]  146 us
    scatter-add x2, other arithmetic, body(): acc_u.at[flat_pick]  143 us
    gather x2, local copies, waits for them, and re-layouts, body(): sel_u = jnp.take(rows_u, pick_blk, axis=0, mode='clip')  83.2 us
    gather x2, local copies, waits for them, and re-layouts, body(): sel_v = jnp.take(rows_v, pick_blk, axis=0, mode='clip')  83.2 us
    scatter-add x2, other arithmetic, device_step(): jnp.zeros((n_local, width), jnp.float32).at[flat_rows]  70.4 us
  transfers between devices with their start and end apart: 4, of which 3 were waited for; matrix products, arithmetic and copies ran while one was open for 2% of the time, Pallas kernels for 0%

commit v1 on v0

v1 whole, which is shorter than its diff:
```python
import functools
import jax
import jax.numpy as jnp
from jax import lax
from jax.experimental import pallas as pl
from jax.experimental.pallas import tpu as pltpu
from jax.sharding import PartitionSpec as P

F32 = jnp.float32
BF16 = jnp.bfloat16
VMEM_LIMIT = 60 * 1024 * 1024
MESH = pl.DeviceIdType.MESH
LANES = 128


def partner(index, k):
    out, bit = 0, 1
    while bit <= k or bit < 2:
        old = (index // bit) % 2
        out = out + ((1 - old) if k & bit else old) * bit
        bit *= 2
    return out + (index // bit) * bit


def visit_order(n):
    chips = max(1, n // 2)
    return sorted(range(n), key=lambda k: (max(min(abs(c - (c ^ (k // 2))), chips - abs(c - (c ^ (k // 2)))) for c in range(chips)), k))


def gelu_pair(pre_act):
    cdf_val = 0.5 * (1.0 + lax.erf(pre_act * 0.7071067811865476))
    pdf_val = jnp.exp(-0.5 * pre_act * pre_act) * 0.3989422804014327
    return pre_act * cdf_val, cdf_val + pre_act * pdf_val


def three_terms(val):
    hi = val.astype(BF16)
    rest = val - hi.astype(F32)
    mid = rest.astype(BF16)
    low = (rest - mid.astype(F32)).astype(BF16)
    return jnp.concatenate([hi, mid, low], axis=0)


def exact_dot(val, rhs):
    rows = val.shape[0]
    out = jnp.dot(three_terms(val), rhs, preferred_element_type=F32)
    return out[:rows] + out[rows:2 * rows] + out[2 * rows:]


def nt_dot(lhs, rhs):
    return lax.dot_general(lhs, rhs, (((1,), (1,)), ((), ())), preferred_element_type=F32)


def ids_kernel(table_n, pool, wanted_ref, pick_ref, gate_ref, ids_ref, gt_ref, out_buf, land, pick_t, gate_t, send_sem, recv_sem):
    me = lax.axis_index('table')
    others = range(1, table_n)
    barrier = pltpu.get_barrier_semaphore()
    for k in others:
        pl.semaphore_signal(barrier, inc=1, device_id={'table': partner(me, k)}, device_id_type=MESH)
    for e in range(table_n):
        out_buf[e, :, 0:pool] = wanted_ref[:, e * pool:(e + 1) * pool]
    land[me] = out_buf[me]
    pl.semaphore_wait(barrier, table_n - 1)
    copies = []
    for k in others:
        to = partner(me, k)
        copies.append(pltpu.make_async_remote_copy(src_ref=out_buf.at[to], dst_ref=land.at[me], send_sem=send_sem.at[k], recv_sem=recv_sem.at[k], device_id={'table': to}, device_id_type=MESH))
        copies[-1].start()

    toks, heads, topk = pick_ref.shape
    for h in range(heads):
        pick_t[h * topk:(h + 1) * topk, :] = pick_ref[:, h, :].astype(F32).T
        gate_t[h * topk:(h + 1) * topk, :] = gate_ref[:, h, :].T
    entries = gt_ref.shape[0]
    entry = lax.broadcasted_iota(jnp.int32, (entries, toks), 0).astype(F32)

    def add_gate(i, acc):
        for j in range(8):
            s = i * 8 + j
            acc = acc + jnp.where(entry == pick_t[pl.ds(s, 1), :], gate_t[pl.ds(s, 1), :], 0.0)
        return acc
    gt_ref[...] = lax.fori_loop(0, heads * topk // 8, add_gate, jnp.zeros((entries, toks), F32))
    for one in copies:
        one.wait()
    ids_ref[...] = land[...]


def share_ids(wanted, pick, gate, table_n, pool):
    toks, heads, topk = pick.shape
    vm = pl.BlockSpec(memory_space=pltpu.VMEM)
    return pl.pallas_call(
        functools.partial(ids_kernel, table_n, pool),
        out_shape=(jax.ShapeDtypeStruct((table_n, 1, LANES), jnp.int32), jax.ShapeDtypeStruct((table_n * pool, toks), F32)),
        in_specs=[vm] * 3,
        out_specs=(vm, vm),
        scratch_shapes=[
            pltpu.VMEM((table_n, 1, LANES), jnp.int32),
            pltpu.VMEM((table_n, 1, LANES), jnp.int32),
            pltpu.VMEM((heads * topk, toks), F32),
            pltpu.VMEM((heads * topk, toks), F32),
            pltpu.SemaphoreType.DMA((table_n,)),
            pltpu.SemaphoreType.DMA((table_n,)),
        ],
        compiler_params=pltpu.CompilerParams(collective_id=0, has_side_effects=True, vmem_limit_bytes=VMEM_LIMIT),
        name="share_ids",
    )(wanted, pick, gate)


def fetch_kernel(table_n, pool, n_local, ids_ref, u_ref, v_ref, rows_ref, tiles, sem):
    first = lax.axis_index('table') * n_local
    for owner in range(table_n):
        def start(i, carry, owner=owner):
            tile = lax.shift_right_logical(ids_ref[owner, 0, i] - first, 3)
            pltpu.make_async_copy(u_ref.at[tile], tiles.at[owner, 0, i], sem.at[owner]).start()
            pltpu.make_async_copy(v_ref.at[tile], tiles.at[owner, 1, i], sem.at[owner]).start()
            return carry
        lax.fori_loop(0, pool, start, 0, unroll=True)

    width = u_ref.shape[2]
    sub = lax.broadcasted_iota(jnp.int32, (8, width), 0)
    for owner in range(table_n):
        pltpu.make_async_copy(tiles.at[owner], tiles.at[owner], sem.at[owner]).wait()
        for which in range(2):
            def pull(g, carry, owner=owner, which=which):
                out = jnp.zeros((8, width), F32)
                for i in range(8):
                    k = g * 8 + i
                    line = jnp.bitwise_and(ids_ref[owner, 0, k] - first, 7)
                    turned = pltpu.roll(tiles[owner, which, k].astype(F32), jnp.bitwise_and(i - line + 8, 7), 0)
                    out = jnp.where(sub == i, turned, out)
                rows_ref[owner, which, pl.ds(pl.multiple_of(g * 8, 8), 8), :] = out.astype(BF16)
                return carry
            lax.fori_loop(0, pool // 8, pull, 0)


def fetch(ids, u_tiles, v_tiles, table_n, pool):
    width = u_tiles.shape[2]
    hbm = pl.BlockSpec(memory_space=pl.ANY)
    return pl.pallas_call(
        functools.partial(fetch_kernel, table_n, pool, u_tiles.shape[0] * 8),
        out_shape=jax.ShapeDtypeStruct((table_n, 2, pool, width), BF16),
        in_specs=[pl.BlockSpec(memory_space=pltpu.SMEM), hbm, hbm],
        out_specs=pl.BlockSpec(memory_space=pltpu.VMEM),
        scratch_shapes=[pltpu.VMEM((table_n, 2, pool, 8, width), BF16), pltpu.SemaphoreType.DMA((table_n,))],
        compiler_params=pltpu.CompilerParams(vmem_limit_bytes=VMEM_LIMIT),
        name="fetch_rows",
    )(ids, u_tiles, v_tiles)


def exchange_kernel(table_n, data_n, pool, send_ref, x_ref, dy_ref, gt_ref, ids_ref,
                    y_ref, dx_ref, own_u, own_v, prev_u, prev_v, next_u, next_v, ids_out,
                    rows_in, part, own, w_all, c_all,
                    a_send, a_recv, b_send, b_recv, c_send, c_recv, i_send, i_recv, o_sem):
    me = lax.axis_index('table')
    row = lax.axis_index('data')
    after, before, across = (row + 1) % data_n, (row + data_n - 1) % data_n, (row + 2) % data_n
    others = [k for k in visit_order(table_n) if k]
    along = (after, before, across)
    barrier = pltpu.get_barrier_semaphore()
    for k in others:
        pl.semaphore_signal(barrier, inc=1, device_id={'table': partner(me, k)}, device_id_type=MESH)
    for to in along:
        pl.semaphore_signal(barrier, inc=1, device_id={'data': to}, device_id_type=MESH)
    pl.semaphore_wait(barrier, len(others) + len(along))

    def remote(src, dst, sem_s, sem_r, **to):
        copy = pltpu.make_async_remote_copy(src_ref=src, dst_ref=dst, send_sem=sem_s, recv_sem=sem_r, device_id=to, device_id_type=MESH)
        copy.start()
        return copy

    copies_a, copies_b, copies_c, local = {}, {}, [], []
    for k in others:
        to = partner(me, k)
        copies_a[k] = remote(send_ref.at[to], rows_in.at[k], a_send.at[k], a_recv.at[k], table=to)
    for j, to in enumerate(along):
        copies_c.append(remote(ids_ref, ids_out.at[j + 1], i_send.at[j], i_recv.at[j], data=to))
    local.append(pltpu.make_async_copy(ids_ref, ids_out.at[0], o_sem.at[0]))
    local[-1].start()

    def spread_on(k):
        e = partner(me, k)
        if k:
            copies_b[k].wait_recv()
        for w, (mine, prev, nxt) in enumerate(((own_u, prev_u, next_u), (own_v, prev_v, next_v))):
            copies_c.append(remote(own.at[e, w], prev.at[e], c_send.at[k, w], c_recv.at[k, w], data=after))
            copies_c.append(remote(own.at[e, w], nxt.at[e], c_send.at[k, 2 + w], c_recv.at[k, 2 + w], data=before))
        for w, mine in enumerate((own_u, own_v)):
            local.append(pltpu.make_async_copy(own.at[e, w], mine.at[e], o_sem.at[1 + 2 * k + w]))
            local[-1].start()

    x = x_ref[...]
    dy = dy_ref[...]
    order = [0] + others
    lag = 2
    for i, k in enumerate(order):
        e = partner(me, k)
        if k:
            copies_a[k].wait_recv()
        else:
            rows_in[0] = send_ref[me]
        pre = nt_dot(rows_in[k, 0], x)
        v_dy = nt_dot(rows_in[k, 1], dy)
        act, slope = gelu_pair(pre)
        gate = gt_ref[pl.ds(pl.multiple_of(e * pool, pool), pool), :]
        weight = gate * act
        coef = gate * slope * v_dy
        w_all[k * pool:(k + 1) * pool, :] = weight
        c_all[k * pool:(k + 1) * pool, :] = coef
        part_u = exact_dot(coef, x).astype(BF16)
        part_v = exact_dot(weight, dy).astype(BF16)
        if k:
            part[k, 0] = part_u
            part[k, 1] = part_v
            copies_b[k] = remote(part.at[k], own.at[me], b_send.at[k], b_recv.at[k], table=e)
        else:
            own[me, 0] = part_u
            own[me, 1] = part_v
            spread_on(0)
        if i > lag:
            spread_on(order[i - lag])
    for k in order[-lag:]:
        spread_on(k)

    width = x_ref.shape[1]
    y_ref[...] = exact_dot(w_all[...].T, rows_in[:, 1].reshape(table_n * pool, width)).astype(BF16)
    dx_ref[...] = exact_dot(c_all[...].T, rows_in[:, 0].reshape(table_n * pool, width)).astype(BF16)

    for k in others:
        copies_a[k].wait_send()
        copies_b[k].wait_send()
    for one in copies_c:
        one.wait()
    for one in local:
        one.wait()


def exchange(rows, x, dy, gt, ids, table_n, data_n, pool):
    toks, width = x.shape
    entries = table_n * pool
    vm = pl.BlockSpec(memory_space=pltpu.VMEM)
    hbm = pl.BlockSpec(memory_space=pl.ANY)
    block = jax.ShapeDtypeStruct((table_n, pool, width), BF16)
    tok_shape = jax.ShapeDtypeStruct((toks, width), BF16)
    dma = pltpu.SemaphoreType.DMA
    return pl.pallas_call(
        functools.partial(exchange_kernel, table_n, data_n, pool),
        out_shape=(tok_shape, tok_shape) + (block,) * 6 + (jax.ShapeDtypeStruct((4, table_n, 1, LANES), jnp.int32),),
        in_specs=[vm] * 5,
        out_specs=(vm, vm) + (hbm,) * 7,
        scratch_shapes=[
            pltpu.VMEM((table_n, 2, pool, width), BF16),
            pltpu.VMEM((table_n, 2, pool, width), BF16),
            pltpu.VMEM((table_n, 2, pool, width), BF16),
            pltpu.VMEM((entries, toks), F32),
            pltpu.VMEM((entries, toks), F32),
            dma((table_n,)), dma((table_n,)), dma((table_n,)), dma((table_n,)),
            dma((table_n, 4)), dma((table_n, 4)), dma((3,)), dma((3,)), dma((2 * table_n + 1,)),
        ],
        compiler_params=pltpu.CompilerParams(collective_id=1, has_side_effects=True, vmem_limit_bytes=VMEM_LIMIT),
        name="exchange",
    )(rows, x, dy, gt, ids)


def spread(row):
    n = row.shape[1]
    return jnp.concatenate([jnp.broadcast_to(row[:, c * 128:(c + 1) * 128], (128, 128)).T for c in range(n // 128)], axis=0)


def fill_kernel(pool, n_local, ids_ref, du_ref, dv_ref, dest_ref, list_ref, zero, zsem):
    tiles_n = du_ref.shape[0]
    fill = zero.shape[0]
    n = dest_ref.shape[1]
    zero[...] = jnp.zeros_like(zero)
    copies = []
    for ref in (du_ref, dv_ref):
        for i in range(tiles_n // fill):
            copies.append(pltpu.make_async_copy(zero, ref.at[pl.ds(i * fill, fill)], zsem.at[len(copies)]))
            copies[-1].start()

    per = LANES // pool
    first = lax.axis_index('table') * n_local
    lane = lax.broadcasted_iota(jnp.int32, (1, LANES), 1)
    table_n = ids_ref.shape[1]
    chunks = []
    for c in range(n // LANES):
        out = None
        for j in range(per):
            b = c * per + j
            piece = ids_ref[b // table_n, b % table_n]
            if j:
                piece = pltpu.roll(piece, j * pool, 1)
                out = jnp.where(lane >= j * pool, piece, out)
            else:
                out = piece
        chunks.append(out - first)
    ids_i = jnp.concatenate(chunks, axis=1)
    row = lax.shift_right_logical(ids_i, 3).astype(F32)
    line = jnp.bitwise_and(ids_i, 7).astype(F32)
    col = spread(row)
    k_row = lax.broadcasted_iota(jnp.int32, (1, n), 1).astype(F32)
    k_col = lax.broadcasted_iota(jnp.int32, (LANES, LANES), 0).astype(F32)

    def over(fn):
        outs = []
        for c in range(n // LANES):
            acc = jnp.zeros((8, LANES), F32)
            for b in range(n // LANES):
                acc = acc + fn(b, c).reshape(LANES // 8, 8, LANES).sum(0)
            outs.append(acc.sum(0, keepdims=True))
        return jnp.concatenate(outs, axis=1)

    def down(val, b):
        return val[b * LANES:(b + 1) * LANES, :]

    def side(val, c):
        return val[:, c * LANES:(c + 1) * LANES]

    leader = over(lambda b, c: jnp.where((down(col, b) == side(row, c)) & (k_col + float(b * LANES) < side(k_row, c)), 1.0, 0.0)) == 0.0
    lead_col = spread(jnp.where(leader, row, 1e9))
    rank = over(lambda b, c: jnp.where(down(lead_col, b) < side(row, c), 1.0, 0.0))
    dest_ref[...] = rank * 8.0 + line
    rank_col = spread(jnp.where(leader, rank, -1.0))
    tiles = over(lambda b, c: jnp.where(down(rank_col, b) == side(k_row, c), down(col, b), 0.0))
    count = jnp.sum(jnp.where(leader, 1.0, 0.0), axis=1, keepdims=True)
    for c in range(n // LANES):
        list_ref[c:c + 1, :] = side(tiles, c).astype(jnp.int32)
    list_ref[n // LANES:n // LANES + 8, :] = jnp.broadcast_to(count, (8, LANES)).astype(jnp.int32)
    for one in copies:
        one.wait()


def fill(ids, tiles_n, width, pool):
    n = ids.shape[0] * ids.shape[1] * pool
    vm = pl.BlockSpec(memory_space=pltpu.VMEM)
    hbm = pl.BlockSpec(memory_space=pl.ANY)
    step = 128
    return pl.pallas_call(
        functools.partial(fill_kernel, pool, tiles_n * 8),
        out_shape=(jax.ShapeDtypeStruct((tiles_n, 8, width), BF16),) * 2 + (jax.ShapeDtypeStruct((1, n), F32), jax.ShapeDtypeStruct((n // LANES + 8, LANES), jnp.int32)),
        in_specs=[vm],
        out_specs=(hbm, hbm, vm, vm),
        scratch_shapes=[pltpu.VMEM((step, 8, width), BF16), pltpu.SemaphoreType.DMA((2 * tiles_n // step,))],
        compiler_params=pltpu.CompilerParams(vmem_limit_bytes=VMEM_LIMIT),
        cost_estimate=pl.CostEstimate(flops=0, bytes_accessed=2 * tiles_n * 8 * width * 2, transcendentals=0),
        name="zero_tables",
    )(ids)


def tiles_kernel(list_ref, dest_ref, *refs):
    parts_u, parts_v = refs[0:4], refs[4:8]
    du_ref, dv_ref, stage, wsem = refs[10:14]
    n = dest_ref.shape[1]
    width = du_ref.shape[2]
    total = list_ref[n // LANES, 0]
    span = 256
    per = span // 8
    piece = n // 4
    target = lax.broadcasted_iota(jnp.int32, (span, n), 0).astype(F32)

    def build(c, carry):
        spot = target + (c * span).astype(F32)
        pick = jnp.where(spot == dest_ref[...], 1.0, 0.0).astype(BF16)
        for which, parts in enumerate((parts_u, parts_v)):
            acc = None
            for j in range(4):
                val = jnp.dot(pick[:, j * piece:(j + 1) * piece], parts[j][...].reshape(piece, width), preferred_element_type=F32)
                acc = val if acc is None else acc + val
            stage[which, pl.ds(c * per, per)] = acc.astype(BF16).reshape(per, 8, width)

        def put(q, inner):
            tile = list_ref[lax.div(q, LANES), lax.rem(q, LANES)]
            pltpu.make_async_copy(stage.at[0, q], du_ref.at[tile], wsem).start()
            pltpu.make_async_copy(stage.at[1, q], dv_ref.at[tile], wsem).start()
            return inner
        lax.fori_loop(c * per, jnp.minimum(total, (c + 1) * per), put, 0)
        return carry
    lax.fori_loop(0, lax.div(total + per - 1, per), build, 0)

    def put_wait(q, carry):
        pltpu.make_async_copy(stage.at[0, q], du_ref.at[0], wsem).wait()
        pltpu.make_async_copy(stage.at[1, q], dv_ref.at[0], wsem).wait()
        return carry
    lax.fori_loop(0, total, put_wait, 0)


def write_tiles(lst, dest, parts_u, parts_v, zero_u, zero_v):
    n = dest.shape[1]
    tiles_n, _, width = zero_u.shape
    vm = pl.BlockSpec(memory_space=pltpu.VMEM)
    hbm = pl.BlockSpec(memory_space=pl.ANY)
    return pl.pallas_call(
        tiles_kernel,
        out_shape=(jax.ShapeDtypeStruct((tiles_n, 8, width), BF16),) * 2,
        in_specs=[pl.BlockSpec(memory_space=pltpu.SMEM)] + [vm] * 9 + [hbm, hbm],
        out_specs=(hbm, hbm),
        scratch_shapes=[pltpu.VMEM((2, n, 8, width), BF16), pltpu.SemaphoreType.DMA],
        input_output_aliases={10: 0, 11: 1},
        compiler_params=pltpu.CompilerParams(vmem_limit_bytes=VMEM_LIMIT),
        name="write_tiles",
    )(lst, dest, *parts_u, *parts_v, zero_u, zero_v)


def solution(mesh):
    table_n = mesh.shape['table']
    data_n = mesh.shape['data']
    tok_spec = P(('replica', 'data', 'table'))
    row_spec = P(('replica', 'table'))
    up = [(i, (i + 1) % data_n) for i in range(data_n)]
    down = [(i, (i + data_n - 1) % data_n) for i in range(data_n)]

    def device_step(tok_loc, dy_loc, u_loc, v_loc, wanted_loc, pick_loc, gate_loc):
        n_local, width = u_loc.shape
        pool = wanted_loc.shape[1] // table_n
        tiles_n = n_local // 8
        ids, gt = share_ids(wanted_loc, pick_loc, gate_loc, table_n, pool)
        rows = fetch(ids, u_loc.reshape(tiles_n, 8, width), v_loc.reshape(tiles_n, 8, width), table_n, pool)
        y_loc, dx_loc, own_u, own_v, prev_u, prev_v, next_u, next_v, all_ids = exchange(rows, tok_loc, dy_loc, gt, ids, table_n, data_n, pool)
        far_u = lax.ppermute(prev_u, 'data', up)
        far_v = lax.ppermute(next_v, 'data', down)
        zero_u, zero_v, dest, lst = fill(all_ids, tiles_n, width, pool)
        grad_u, grad_v = write_tiles(lst, dest, (own_u, prev_u, next_u, far_u), (own_v, prev_v, next_v, far_v), zero_u, zero_v)
        return y_loc, dx_loc, grad_u.reshape(n_local, width), grad_v.reshape(n_local, width)

    return jax.shard_map(device_step, mesh=mesh, in_specs=(tok_spec, tok_spec, row_spec, row_spec, tok_spec, tok_spec, tok_spec), out_specs=(tok_spec, tok_spec, row_spec, row_spec), check_vma=False)
```

time: 2990 us -> 101 us (0.03)
  blocking collectives: 2240 us -> 0 us
  other arithmetic: 420 us -> 0 us
  local copies, waits for them, and re-layouts: 227 us -> 5.73 us
  Pallas kernels: 0 us -> 91.8 us
  matrix products: 53.4 us -> 0 us
    psum x1 -> x0, blocking collectives: 2230 us -> none  [device_step(): grad_u = lax.psum(grad_u, 'data')]
    scatter-add x6 -> x0, other arithmetic: 359 us -> none  [the longest x2 146 us: body(): acc_v.at[flat_pick]]
    gather x6 -> x0, local copies, waits for them, and re-layouts: 174 us -> none  [the longest x2 83.2 us: body(): sel_u = jnp.take(rows_u, pick_blk, axis=0, mode='clip')]
    pallas_call x0 -> x5, Pallas kernels: none -> 91.8 us  [the longest x1 44.2 us: exchange(): pl.pallas_call(functools.partial(exchange_kernel, table_n, data_n, pool),...]
    dot_general x8 -> x0, matrix products: 53.4 us -> none  [the longest x2 16.4 us: body(): jnp.einsum('bs,bsd->bd', coef_sel, sel_u, preferred_element_type=jnp.floa...]
    mul x7 -> x0, other arithmetic: 47.3 us -> none  [the longest x2 22.7 us: body(): coef_sel[:, :, None] * x_blk[:, None, :]]
    another operation x2 -> x0, local copies, waits for them, and re-layouts: 42.6 us -> none
  transfers between devices with their start and end apart: 4 -> 2, of which waited for: 3 -> 0; matrix products, arithmetic and copies ran while one was open for 2% -> 0% of each run, Pallas kernels for 0% -> 24%
where the time goes in v1:
time: 101 us
  Pallas kernels  91.8 us (91%)
  local copies, waits for them, and re-layouts  5.73 us (6%)
  starting transfers between devices  2.76 us (3%)
    pallas_call x1, Pallas kernels, exchange(): pl.pallas_call(functools.partial(exchange_kernel, table_n, data_n, pool),...  44.2 us
    pallas_call x1, Pallas kernels, fill(): pl.pallas_call(functools.partial(fill_kernel, pool, tiles_n * 8), out_sha...  24.5 us
    pallas_call x1, Pallas kernels, share_ids(): pl.pallas_call(functools.partial(ids_kernel, table_n, pool), out_shape=(j...  8.81 us
    pallas_call x1, Pallas kernels, write_tiles(): pl.pallas_call(tiles_kernel, out_shape=(jax.ShapeDtypeStruct((tiles_n, 8,...  7.59 us
    pallas_call x1, Pallas kernels, fetch(): pl.pallas_call(functools.partial(fetch_kernel, table_n, pool, u_tiles.sha...  6.77 us
    unnamed x12, local copies, waits for them, and re-layouts  5.73 us
    ppermute x1, starting transfers between devices, device_step(): far_v = lax.ppermute(next_v, 'data', down)  2.65 us
  transfers between devices with their start and end apart: 2, of which 0 were waited for; matrix products, arithmetic and copies ran while one was open for 0% of the time, Pallas kernels for 24%

profile of v1, /device:TPU:97, one launch (start us, length us, event | category | flops | bytes accessed | tf_op | source)
XLA Modules:
  0.0 101.0 jit_solution(131364760218292762)
XLA Ops:
  0.6 1.7 %copy.13.pick_ref = s32[128,4,32]{2,1,0:T(4,128)} copy(s32[128,4,32]{0,2,1:T(8,128)} %param.12) | data formatting | bytes 131072 | tf_op args[5]
  2.3 1.7 %copy.14.gate_ref = f32[128,4,32]{2,1,0:T(4,128)} copy(f32[128,4,32]{0,2,1:T(8,128)} %param.13) | data formatting | bytes 131072 | tf_op args[6]
  4.0 8.8 %share_ids.1 = (s32[8,1,128]{2,1,0:T(1,128)}, f32[256,128]{1,0:T(8,128)}) custom-call(s32[1,256]{1,0:T(1,128)} %wanted_ref.1, s32[128,4,32]{2,1,0:T(4,128)} %copy.13.pick_ref, f32[128,4,32]{2,1,0:T(4,128)} %copy.14.gate_ref), custom_call_target="tpu_custom_call" | custom-call | tf_op jit(solution)/shard_map/share_ids/pallas_call | solution.py:91
  12.8 6.8 %fetch_rows.1.send_ref = bf16[8,2,32,1024]{3,2,1,0:T(8,128)(2,1)} custom-call(s32[8,1,128]{2,1,0:T(1,128)} %get-tuple-element.21.ids_ref, bf16[2048,8,1024]{2,1,0:T(8,128)(2,1)} %bitcast.6, bf16[2048,8,1024]{2,1,0:T(8,128)(2,1)} %bitcast.7), custom_call_target="tpu_custom_call" | custom-call | tf_op jit(solution)/shard_map/fetch_rows/pallas_call | solution.py:139
  19.6 44.2 %exchange.1 = (bf16[128,1024]{1,0:T(8,128)(2,1)}, bf16[128,1024]{1,0:T(8,128)(2,1)}, bf16[8,32,1024]{2,1,0:T(8,128)(2,1)}, bf16[8,32,1024]{2,1,0:T(8,128)(2,1)},...) custom-call(bf16[8,2,32,1024]{3,2,1,0:T(8,128)(2,1)} %fetch_rows.1.s, ...), custom_call_target="tpu_custom_call" | custom-call | tf_op jit(solution)/shard_map/exchange/pallas_call | solution.py:245
  63.8 0.1 collective-permute-start
  63.9 2.7 %collective-permute-start.1 = (bf16[8,32,1024]{2,1,0:T(8,128)(2,1)}, bf16[8,32,1024]{2,1,0:T(8,128)(2,1)S(1)}, u32[]{:S(2)}, u32[]{:S(2)}) collective-permute-start(bf16[8,32,1024]{2,1,0:T(8,128)(2,1)} %get-tuple-element.33.refs_6_), channel_id=1, source_target_pairs={{0,24},{8,0},{16,8},{24,16},{1,25},{9,1},{17,9},{25,17},{2,26},{10... | collective-permute-start | bytes 1572872 | tf_op jit(solution)/shard_map/ppermute | solution.py:419
  66.5 24.5 %zero_tables.1 = (bf16[2048,8,1024]{2,1,0:T(8,128)(2,1)}, bf16[2048,8,1024]{2,1,0:T(8,128)(2,1)}, f32[1,1024]{1,0:T(1,128)}, s32[16,128]{1,0:T(8,128)}) custom-call(s32[4,8,1,128]{3,2,1,0:T(1,128)} %get-tuple-element.25.ids_ref), custom_call_target="tpu_custom_call" | custom-call | bytes 67108864 | tf_op jit(solution)/shard_map/zero_tables/pallas_call | solution.py:337
  91.0 0.0 collective-permute-done.refs_3_
  91.0 0.0 copy-start
  91.0 0.0 collective-permute-done.1.refs_7_
  91.0 0.0 copy-start.1
  91.0 0.8 copy-done
  91.8 0.2 copy-done.1
  92.0 0.0 copy-start.3
  92.0 0.0 copy-start.2
  92.0 7.6 %write_tiles.1 = (bf16[2048,8,1024]{2,1,0:T(8,128)(2,1)}, bf16[2048,8,1024]{2,1,0:T(8,128)(2,1)}) custom-call(s32[16,128]{1,0:T(8,128)} %get-tuple-element.26.list_ref, f32[1,1024]{1,0:T(1,128)} %get-tuple-element.27.dest_ref, bf16[8,32,1024]{2,1,0:T(8,128)(2,1)} %get-tuple-element.28.refs_0_, ...), custom_call_target="tpu_custom_call", output_to_operand_aliasing={{0}: (10, {}), {1}: (11, {})} | custom-call | tf_op jit(solution)/shard_map/write_tiles/pallas_call | solution.py:391
  99.6 0.0 copy-done.3
  99.6 0.7 copy.19
  100.3 0.0 copy-done.2
  100.3 0.7 copy.20
Async XLA Ops:
  63.8 27.3 %collective-permute-start = (bf16[8,32,1024]{2,1,0:T(8,128)(2,1)}, bf16[8,32,1024]{2,1,0:T(8,128)(2,1)S(1)}, u32[]{:S(2)}, u32[]{:S(2)}) collective-permute-start(bf16[8,32,1024]{2,1,0:T(8,128)(2,1)} %get-tuple-element.29.refs_1_), channel_id=1, source_target_pairs={{0,8},{8,16},{16,24},{24,0},{1,9},{9,17},{17,25},{25,1},{2,10},{10... | collective-permute-start | bytes 1572872 | tf_op jit(solution)/shard_map/ppermute | solution.py:418
  63.9 27.2 %collective-permute-start.1 = (bf16[8,32,1024]{2,1,0:T(8,128)(2,1)}, bf16[8,32,1024]{2,1,0:T(8,128)(2,1)S(1)}, u32[]{:S(2)}, u32[]{:S(2)}) collective-permute-start(bf16[8,32,1024]{2,1,0:T(8,128)(2,1)} %get-tuple-element.33.refs_6_), channel_id=1, source_target_pairs={{0,24},{8,0},{16,8},{24,16},{1,25},{9,1},{17,9},{25,17},{2,26},{10... | collective-permute-start | bytes 1572872 | tf_op jit(solution)/shard_map/ppermute | solution.py:419
  91.0 0.8 copy-start
  91.0 1.0 copy-start.1
  92.0 7.6 %copy-start.3 = (bf16[128,1024]{1,0:T(8,128)(2,1)S(1)}, bf16[128,1024]{1,0:T(8,128)(2,1)}, u32[]{:S(2)}) copy-start(bf16[128,1024]{1,0:T(8,128)(2,1)} %get-tuple-element.42) | copy-start | bytes 786436
  92.0 8.3 %copy-start.2 = (bf16[128,1024]{1,0:T(8,128)(2,1)S(1)}, bf16[128,1024]{1,0:T(8,128)(2,1)}, u32[]{:S(2)}) copy-start(bf16[128,1024]{1,0:T(8,128)(2,1)} %get-tuple-element.43) | copy-start | bytes 786436

commit v2 on v1

v2 whole, which is shorter than its diff:
```python
import functools
import jax
import jax.numpy as jnp
from jax import lax
from jax.experimental import pallas as pl
from jax.experimental.pallas import tpu as pltpu
from jax.sharding import PartitionSpec as P

F32 = jnp.float32
BF16 = jnp.bfloat16
MIB = 1024 * 1024
MESH = pl.DeviceIdType.MESH
LANES = 128


def partner(index, k):
    out, bit = 0, 1
    while bit <= k or bit < 2:
        old = (index // bit) % 2
        out = out + ((1 - old) if k & bit else old) * bit
        bit *= 2
    return out + (index // bit) * bit


def visit_order(n):
    chips = max(1, n // 2)
    return sorted(range(n), key=lambda k: (max(min(abs(c - (c ^ (k // 2))), chips - abs(c - (c ^ (k // 2)))) for c in range(chips)), k))


def gelu_pair(pre_act):
    cdf_val = 0.5 * (1.0 + lax.erf(pre_act * 0.7071067811865476))
    pdf_val = jnp.exp(-0.5 * pre_act * pre_act) * 0.3989422804014327
    return pre_act * cdf_val, cdf_val + pre_act * pdf_val


def three_terms(val):
    hi = val.astype(BF16)
    rest = val - hi.astype(F32)
    mid = rest.astype(BF16)
    low = (rest - mid.astype(F32)).astype(BF16)
    return jnp.concatenate([hi, mid, low], axis=0)


def exact_dot(val, rhs):
    rows = val.shape[0]
    out = jnp.dot(three_terms(val), rhs, preferred_element_type=F32)
    return out[:rows] + out[rows:2 * rows] + out[2 * rows:]


def nt_dot(lhs, rhs):
    return lax.dot_general(lhs, rhs, (((1,), (1,)), ((), ())), preferred_element_type=F32)


def ids_kernel(table_n, pool, wanted_ref, ids_ref, out_buf, land, send_sem, recv_sem):
    me = lax.axis_index('table')
    others = range(1, table_n)
    barrier = pltpu.get_barrier_semaphore()
    for k in others:
        pl.semaphore_signal(barrier, inc=1, device_id={'table': partner(me, k)}, device_id_type=MESH)
    for e in range(table_n):
        out_buf[e, :, 0:pool] = wanted_ref[:, e * pool:(e + 1) * pool]
    land[0] = out_buf[me]
    pl.semaphore_wait(barrier, table_n - 1)
    copies = []
    for k in others:
        to = partner(me, k)
        copies.append(pltpu.make_async_remote_copy(src_ref=out_buf.at[to], dst_ref=land.at[k], send_sem=send_sem.at[k], recv_sem=recv_sem.at[k], device_id={'table': to}, device_id_type=MESH))
        copies[-1].start()
    for one in copies:
        one.wait()
    ids_ref[...] = land[...]


def share_ids(wanted, table_n, pool):
    vm = pl.BlockSpec(memory_space=pltpu.VMEM)
    return pl.pallas_call(
        functools.partial(ids_kernel, table_n, pool),
        out_shape=jax.ShapeDtypeStruct((table_n, 1, LANES), jnp.int32),
        in_specs=[vm],
        out_specs=vm,
        scratch_shapes=[
            pltpu.VMEM((table_n, 1, LANES), jnp.int32),
            pltpu.VMEM((table_n, 1, LANES), jnp.int32),
            pltpu.SemaphoreType.DMA((table_n,)),
            pltpu.SemaphoreType.DMA((table_n,)),
        ],
        compiler_params=pltpu.CompilerParams(collective_id=0, has_side_effects=True, vmem_limit_bytes=2 * MIB),
        name="share_ids",
    )(wanted)


def fetch_kernel(table_n, pool, n_local, ids_ref, u_ref, v_ref, rows_ref, tiles, sem):
    first = lax.axis_index('table') * n_local
    for k in range(table_n):
        for i in range(pool):
            tile = lax.shift_right_logical(ids_ref[k, 0, i] - first, 3)
            pltpu.make_async_copy(u_ref.at[tile], tiles.at[k, 0, i], sem.at[k]).start()
            pltpu.make_async_copy(v_ref.at[tile], tiles.at[k, 1, i], sem.at[k]).start()

    width = u_ref.shape[2]
    sub = lax.broadcasted_iota(jnp.int32, (8, width), 0)
    for k in range(table_n):
        pltpu.make_async_copy(tiles.at[k], tiles.at[k], sem.at[k]).wait()

        def pull(g, carry, k=k):
            for which in range(2):
                out = jnp.zeros((8, width), F32)
                for i in range(8):
                    s = g * 8 + i
                    line = jnp.bitwise_and(ids_ref[k, 0, s] - first, 7)
                    turned = pltpu.roll(tiles[k, which, s].astype(F32), jnp.bitwise_and(i - line + 8, 7), 0)
                    out = jnp.where(sub == i, turned, out)
                rows_ref[k, which, pl.ds(pl.multiple_of(g * 8, 8), 8), :] = out.astype(BF16)
            return carry
        lax.fori_loop(0, pool // 8, pull, 0)


def fetch(ids, u_tiles, v_tiles, table_n, pool):
    width = u_tiles.shape[2]
    hbm = pl.BlockSpec(memory_space=pl.ANY)
    return pl.pallas_call(
        functools.partial(fetch_kernel, table_n, pool, u_tiles.shape[0] * 8),
        out_shape=jax.ShapeDtypeStruct((table_n, 2, pool, width), BF16),
        in_specs=[pl.BlockSpec(memory_space=pltpu.SMEM), hbm, hbm],
        out_specs=pl.BlockSpec(memory_space=pltpu.VMEM),
        scratch_shapes=[pltpu.VMEM((table_n, 2, pool, 8, width), BF16), pltpu.SemaphoreType.DMA((table_n,))],
        compiler_params=pltpu.CompilerParams(vmem_limit_bytes=40 * MIB),
        name="fetch_rows",
    )(ids, u_tiles, v_tiles)


PLAN = "a1 a2 a6 a3 a7 s0 i0 w1 s1 w2 w6 a4 w3 w7 a5 s2 s6 s3 s7 w4 w5 x4 x5"


def plan_of(order, early):
    if order == [0, 1, 2, 3, 6, 7, 4, 5] and early == 6:
        return PLAN.split()
    others = order[1:]
    return [f"a{k}" for k in others] + ["s0", "i0"] + [f"w{k}" for k in others] + [("s" if k in order[:early] else "x") + str(k) for k in others]


def split_of(table_n):
    return table_n - table_n // 4


def exchange_kernel(table_n, data_n, pool, send_ref, x_ref, dy_ref, pick_ref, gate_ref, ids_ref,
                    w_all, c_all, rows_in, own_u, own_v, to_next, prev_v, next_u, to_prev, late, ids_out,
                    part,
                    a_send, a_recv, b_send, b_recv, c_send, c_recv, i_send, i_recv):
    me = lax.axis_index('table')
    row = lax.axis_index('data')
    after, before, across = (row + 1) % data_n, (row + data_n - 1) % data_n, (row + 2) % data_n
    order = visit_order(table_n)
    early = split_of(table_n)
    spot = {k: p for p, k in enumerate(order)}
    others = order[1:]
    along = (after, before, across)
    barrier = pltpu.get_barrier_semaphore()
    for k in others:
        pl.semaphore_signal(barrier, inc=1, device_id={'table': partner(me, k)}, device_id_type=MESH)
    for to in along:
        pl.semaphore_signal(barrier, inc=1, device_id={'data': to}, device_id_type=MESH)
    def remote(src, dst, sem_s, sem_r, **to):
        copy = pltpu.make_async_remote_copy(src_ref=src, dst_ref=dst, send_sem=sem_s, recv_sem=sem_r, device_id=to, device_id_type=MESH)
        copy.start()
        return copy

    copies_a, copies_b, copies_c = {}, {}, []
    x = x_ref[...]
    dy = dy_ref[...]

    def home(k, w):
        p = spot[k]
        return (own_u, own_v)[w].at[p] if p < early else late.at[w, p - early]

    def ask(k):
        copies_a[k] = remote(send_ref.at[k], rows_in.at[spot[k]], a_send.at[k], a_recv.at[k], table=partner(me, k))

    def share(k):
        for j, to in enumerate(along):
            copies_c.append(remote(ids_ref, ids_out.at[j + 1], i_send.at[j], i_recv.at[j], data=to))
        ids_out[0] = ids_ref[...]

    def gates_of(e):
        toks = x.shape[0]
        entry = (lax.broadcasted_iota(jnp.int32, (pool, toks), 0) + e * pool).astype(F32)
        accs = [jnp.zeros((pool, toks), F32) for _ in range(2)]

        def add_gate(i, accs):
            accs = list(accs)
            for j in range(16):
                s = i * 16 + j
                accs[j % 2] = accs[j % 2] + jnp.where(entry == pick_ref[pl.ds(s, 1), :].astype(F32), gate_ref[pl.ds(s, 1), :], 0.0)
            return tuple(accs)
        accs = lax.fori_loop(0, pick_ref.shape[0] // 16, add_gate, tuple(accs))
        return accs[0] + accs[1]

    def spread_on(k):
        p = spot[k]
        for w, (prev, nxt) in enumerate(((to_next, next_u), (prev_v, to_prev))):
            if k:
                copies_b[k, w].wait_recv()
            copies_c.append(remote(home(k, w), prev.at[p], c_send.at[k, w], c_recv.at[k, w], data=after))
            copies_c.append(remote(home(k, w), nxt.at[p], c_send.at[k, 2 + w], c_recv.at[k, 2 + w], data=before))

    def hold(k):
        p = spot[k] - early
        for w in range(2):
            copies_b[k, w].wait_recv()
            for out in (to_next, to_prev):
                out[early + w * (table_n - early) + p] = late[w, p]

    def work(k):
        e = partner(me, k)
        p = spot[k]
        gate = gates_of(e)
        if k:
            copies_a[k].wait_recv()
        else:
            rows_in[p] = send_ref[k]
        pre = nt_dot(rows_in[p, 0], x)
        v_dy = nt_dot(rows_in[p, 1], dy)
        act, slope = gelu_pair(pre)
        weight = gate * act
        coef = gate * slope * v_dy
        w_all[p * pool:(p + 1) * pool, :] = weight
        c_all[p * pool:(p + 1) * pool, :] = coef
        for w, val in enumerate((exact_dot(coef, x), exact_dot(weight, dy))):
            if k:
                part[k, w] = val.astype(BF16)
                copies_b[k, w] = remote(part.at[k, w], home(k, w), b_send.at[k, w], b_recv.at[k, w], table=e)
            else:
                home(k, w)[...] = val.astype(BF16)

    work(0)
    pl.semaphore_wait(barrier, len(others) + len(along))
    for step in plan_of(order, early):
        {'a': ask, 'w': work, 's': spread_on, 'x': hold, 'i': share}[step[0]](int(step[1:]))

    for k in others:
        copies_a[k].wait_send()
        copies_b[k, 0].wait_send()
        copies_b[k, 1].wait_send()
    for one in copies_c:
        one.wait()


def exchange(rows, x, dy, pick, gate, ids, table_n, data_n, pool):
    toks, width = x.shape
    entries = table_n * pool
    vm = pl.BlockSpec(memory_space=pltpu.VMEM)
    hbm = pl.BlockSpec(memory_space=pl.ANY)
    early = split_of(table_n)
    block = jax.ShapeDtypeStruct((early, pool, width), BF16)
    pack = jax.ShapeDtypeStruct((2 * table_n - early, pool, width), BF16)
    factor = jax.ShapeDtypeStruct((entries, toks), F32)
    both = (table_n, 2, pool, width)
    dma = pltpu.SemaphoreType.DMA
    return pl.pallas_call(
        functools.partial(exchange_kernel, table_n, data_n, pool),
        out_shape=(factor, factor, jax.ShapeDtypeStruct(both, BF16)) + (block, block, pack, block, block, pack) + (jax.ShapeDtypeStruct((2, table_n - early, pool, width), BF16), jax.ShapeDtypeStruct((4, table_n, 1, LANES), jnp.int32)),
        in_specs=[vm] * 6,
        out_specs=(vm,) * 11,
        scratch_shapes=[
            pltpu.VMEM(both, BF16),
            dma((table_n,)), dma((table_n,)), dma((table_n, 2)), dma((table_n, 2)),
            dma((table_n, 4)), dma((table_n, 4)), dma((3,)), dma((3,)),
        ],
        compiler_params=pltpu.CompilerParams(collective_id=1, has_side_effects=True, vmem_limit_bytes=16 * MIB),
        name="exchange",
    )(rows, x, dy, pick, gate, ids)


def blocks_of(table_n):
    order = visit_order(table_n)
    early, last = order[:split_of(table_n)], order[split_of(table_n):]
    near = [(0, k) for k in early + last] + [(s, k) for s in (1, 2) for k in early]
    return near + [(s, k) for s in (1, 2, 3) for k in last] + [(3, k) for k in early], len(near)


def stack(blocks):
    return jnp.concatenate([b.reshape(-1, b.shape[-1]) for b in blocks], axis=0)


def spread(row):
    n = row.shape[1]
    return jnp.concatenate([jnp.broadcast_to(row[:, c * 128:(c + 1) * 128], (128, 128)).T for c in range(n // 128)], axis=0)


def fill_kernel(pool, n_local, ids_ref, w_ref, c_ref, rows_ref, own_u, own_v, to_next, prev_v, next_u, to_prev, late,
                du_ref, dv_ref, y_ref, dx_ref, sum_u, sum_v, rank_ref, spot_ref, list_ref,
                zero, zsem):
    tiles_n = du_ref.shape[0]
    step = zero.shape[0]
    n = rank_ref.shape[1]
    width = du_ref.shape[2]
    zero[...] = jnp.zeros_like(zero)

    def start(i, carry):
        for w, ref in enumerate((du_ref, dv_ref)):
            pltpu.make_async_copy(zero, ref.at[pl.ds(i * step, step)], zsem.at[w]).start()
        return carry
    lax.fori_loop(0, tiles_n // step, start, 0)

    per = LANES // pool
    first = lax.axis_index('table') * n_local
    lane = lax.broadcasted_iota(jnp.int32, (1, LANES), 1)
    table_n = ids_ref.shape[1]
    blocks, n_near = blocks_of(table_n)
    near = n_near * pool
    chunks = []
    for c in range(n // LANES):
        out = None
        for j in range(per):
            piece = ids_ref[blocks[c * per + j]]
            if j:
                piece = pltpu.roll(piece, j * pool, 1)
                out = jnp.where(lane >= j * pool, piece, out)
            else:
                out = piece
        chunks.append(out - first)
    ids_i = jnp.concatenate(chunks, axis=1)
    row = ids_i.astype(F32)
    tile = lax.shift_right_logical(ids_i, 3).astype(F32)
    line = jnp.bitwise_and(ids_i, 7).astype(F32)
    row_col = spread(row)
    tile_col = spread(tile)
    k_row = lax.broadcasted_iota(jnp.int32, (1, n), 1).astype(F32)
    k_col = lax.broadcasted_iota(jnp.int32, (LANES, LANES), 0).astype(F32)

    def over(fn, wide=n):
        outs = []
        for c in range(wide // LANES):
            acc = jnp.zeros((8, LANES), F32)
            for b in range(n // LANES):
                acc = acc + fn(b, c).reshape(LANES // 8, 8, LANES).sum(0)
            outs.append(acc.sum(0, keepdims=True))
        return jnp.concatenate(outs, axis=1)

    def down(val, b):
        return val[b * LANES:(b + 1) * LANES, :]

    def side(val, c):
        return val[:, c * LANES:(c + 1) * LANES]

    def ranked(val, col):
        earlier = over(lambda b, c: jnp.where((down(col, b) == side(val, c)) & (k_col + float(b * LANES) < side(k_row, c)), 1.0, 0.0))
        leader = earlier == 0.0
        lead_col = spread(jnp.where(leader, val, 1e9))
        return leader, over(lambda b, c: jnp.where(down(lead_col, b) < side(val, c), 1.0, 0.0))

    row_leader, rank = ranked(row, row_col)
    tile_leader, tile_rank = ranked(tile, tile_col)
    rank_col = spread(jnp.where(row_leader, rank, -1.0))
    tile_rank_col = spread(jnp.where(tile_leader, tile_rank, -1.0))
    spot_col = spread(tile_rank * 8.0 + line)
    spots = over(lambda b, c: jnp.where(down(rank_col, b) == side(k_row, c), down(spot_col, b), 0.0))
    tiles = over(lambda b, c: jnp.where(down(tile_rank_col, b) == side(k_row, c), down(tile_col, b), 0.0))
    lead_spot_col = spread(jnp.where(row_leader, tile_rank * 8.0 + line, 1e9))
    before = over(lambda b, c: jnp.where(down(lead_spot_col, b) < side(k_row, c) * 256.0, 1.0, 0.0), LANES)
    n_rows = jnp.sum(jnp.where(row_leader, 1.0, 0.0))
    n_tiles = jnp.sum(jnp.where(tile_leader, 1.0, 0.0))
    rank_ref[...] = rank
    lines = n // LANES
    lane_f = lane.astype(F32)
    for c in range(lines):
        spot_ref[c:c + 1, :] = jnp.where(side(k_row, c) < n_rows, side(spots, c), -1.0)
        list_ref[c:c + 1, :] = side(tiles, c).astype(jnp.int32)
    list_ref[lines:lines + 1, :] = jnp.where(lane == 0, n_tiles, n_rows).astype(jnp.int32)
    list_ref[lines + 1:lines + 2, :] = before.astype(jnp.int32)
    list_ref[lines + 2:, :] = jnp.zeros((list_ref.shape[0] - lines - 2, LANES), jnp.int32)

    flat = (table_n * pool, width)
    y_ref[...] = exact_dot(w_ref[...].T, rows_ref[:, 1].reshape(flat)).astype(BF16)
    dx_ref[...] = exact_dot(c_ref[...].T, rows_ref[:, 0].reshape(flat)).astype(BF16)

    target = lax.broadcasted_iota(jnp.int32, (LANES, near), 0).astype(F32)
    n_chunks = lax.div(n_rows.astype(jnp.int32) + (LANES - 1), LANES)

    def add_up(c, carry):
        hot = jnp.where(target + (c * LANES).astype(F32) == rank_ref[:, 0:near], 1.0, 0.0).astype(BF16)
        span = pl.ds(pl.multiple_of(c * LANES, LANES), LANES)
        for w, (out, own, prev, nxt) in enumerate(((sum_u, own_u, to_next, next_u), (sum_v, own_v, prev_v, to_prev))):
            out[span, :] = jnp.dot(hot, stack([own[...], late[w], prev[0:own.shape[0]], nxt[0:own.shape[0]]]), preferred_element_type=F32)
        return carry
    lax.fori_loop(0, n_chunks, add_up, 0)
    for w, ref in enumerate((du_ref, dv_ref)):
        pltpu.make_async_copy(ref, ref, zsem.at[w]).wait()


def fill(ids, w_all, c_all, rows, near, tiles_n, pool):
    table_n = ids.shape[1]
    n = ids.shape[0] * table_n * pool
    entries, toks = w_all.shape
    width = rows.shape[3]
    vm = pl.BlockSpec(memory_space=pltpu.VMEM)
    hbm = pl.BlockSpec(memory_space=pl.ANY)
    step = 128
    tok_shape = jax.ShapeDtypeStruct((toks, width), BF16)
    return pl.pallas_call(
        functools.partial(fill_kernel, pool, tiles_n * 8),
        out_shape=(jax.ShapeDtypeStruct((tiles_n, 8, width), BF16),) * 2 + (tok_shape, tok_shape)
        + (jax.ShapeDtypeStruct((n, width), F32),) * 2
        + (jax.ShapeDtypeStruct((1, n), F32), jax.ShapeDtypeStruct((n // LANES, LANES), F32), jax.ShapeDtypeStruct((n // LANES + 8, LANES), jnp.int32)),
        in_specs=[vm] * 11,
        out_specs=(hbm, hbm) + (vm,) * 7,
        scratch_shapes=[
            pltpu.VMEM((step, 8, width), BF16),
            pltpu.SemaphoreType.DMA((2,)),
        ],
        compiler_params=pltpu.CompilerParams(vmem_limit_bytes=24 * MIB),
        cost_estimate=pl.CostEstimate(flops=0, bytes_accessed=2 * tiles_n * 8 * width * 2, transcendentals=0),
        name="zero_tables",
    )(ids, w_all, c_all, rows, *near)


def tiles_kernel(near, list_ref, rank_ref, spot_ref, from_prev, from_next, late_far, sum_u, sum_v, zero_u, zero_v, du_ref, dv_ref, done, stage, wsem):
    n = rank_ref.shape[1]
    width = du_ref.shape[2]
    lines = n // LANES
    n_tiles = list_ref[lines, 0]
    n_rows = list_ref[lines, 1]
    n_chunks = lax.div(n_rows + (LANES - 1), LANES)
    target = lax.broadcasted_iota(jnp.int32, (LANES, n - near), 0).astype(F32)

    def finish(c, carry):
        span = pl.ds(pl.multiple_of(c * LANES, LANES), LANES)
        hot = jnp.where(target + (c * LANES).astype(F32) == rank_ref[:, near:], 1.0, 0.0).astype(BF16)
        late_n = late_far.shape[1]
        early = from_prev.shape[0] - 2 * late_n
        for w, (far, sums) in enumerate(((from_prev, sum_u), (from_next, sum_v))):
            late = [ref[early + w * late_n:early + (w + 1) * late_n] for ref in (from_prev, from_next)]
            last = jnp.dot(hot, stack(late + [late_far[w], far[0:early]]), preferred_element_type=F32)
            done[w, span, :] = (sums[span, :] + last).astype(BF16)
        return carry
    lax.fori_loop(0, n_chunks, finish, 0)

    tall = 256
    per = tall // 8
    place = lax.broadcasted_iota(jnp.int32, (tall, LANES), 0).astype(F32)

    ring = stage.shape[0]
    n_builds = lax.div(n_tiles + per - 1, per)

    def drain(slot):
        pltpu.make_async_copy(stage.at[slot], stage.at[slot], wsem.at[slot]).wait()

    def build(c, carry):
        slot = lax.rem(c, ring)

        @pl.when(c >= ring)
        def _():
            drain(slot)
        start = lax.div(list_ref[lines + 1, c], LANES)
        end = lax.div(list_ref[lines + 1, c + 1] + (LANES - 1), LANES)

        def lay(kc):
            hot = jnp.where(place + (c * tall).astype(F32) == spot_ref[pl.ds(kc, 1), :], 1.0, 0.0).astype(BF16)
            span = pl.ds(pl.multiple_of(kc * LANES, LANES), LANES)
            return [jnp.dot(hot, done[w, span, :], preferred_element_type=F32).astype(BF16).reshape(per, 8, width) for w in range(2)]
        for w, val in enumerate(lay(start)):
            stage[slot, w] = val

        def more(kc, inner):
            for w, val in enumerate(lay(kc)):
                stage[slot, w] = stage[slot, w] + val
            return inner
        lax.fori_loop(start + 1, end, more, 0)

        def put(q, inner):
            tile = list_ref[lax.div(q, LANES), lax.rem(q, LANES)]
            pltpu.make_async_copy(stage.at[slot, 0, q - c * per], du_ref.at[tile], wsem.at[slot]).start()
            pltpu.make_async_copy(stage.at[slot, 1, q - c * per], dv_ref.at[tile], wsem.at[slot]).start()
            return inner
        lax.fori_loop(c * per, jnp.minimum(n_tiles, (c + 1) * per), put, 0)
        return carry
    lax.fori_loop(0, n_builds, build, 0)

    def full(c, carry):
        drain(lax.rem(c, ring))
        return carry
    lax.fori_loop(jnp.maximum(0, n_builds - ring), n_builds - 1, full, 0)
    slot = lax.rem(n_builds - 1, ring)

    def rest(q, carry):
        for w, ref in enumerate((du_ref, dv_ref)):
            pltpu.make_async_copy(stage.at[slot, w, 0], ref.at[0], wsem.at[slot]).wait()
        return carry
    lax.fori_loop((n_builds - 1) * per, n_tiles, rest, 0)


def write_tiles(lst, rank, spot, far, sum_u, sum_v, zero_u, zero_v, near):
    n = rank.shape[1]
    tiles_n, _, width = zero_u.shape
    vm = pl.BlockSpec(memory_space=pltpu.VMEM)
    hbm = pl.BlockSpec(memory_space=pl.ANY)
    return pl.pallas_call(
        functools.partial(tiles_kernel, near),
        out_shape=(jax.ShapeDtypeStruct((tiles_n, 8, width), BF16),) * 2,
        in_specs=[pl.BlockSpec(memory_space=pltpu.SMEM)] + [vm] * 7 + [hbm] * 2,
        out_specs=(hbm, hbm),
        scratch_shapes=[
            pltpu.VMEM((2, n, width), BF16),
            pltpu.VMEM((8, 2, 32, 8, width), BF16),
            pltpu.SemaphoreType.DMA((8,)),
        ],
        input_output_aliases={8: 0, 9: 1},
        compiler_params=pltpu.CompilerParams(vmem_limit_bytes=24 * MIB),
        name="write_tiles",
    )(lst, rank, spot, *far, sum_u, sum_v, zero_u, zero_v)


def solution(mesh):
    table_n = mesh.shape['table']
    data_n = mesh.shape['data']
    tok_spec = P(('replica', 'data', 'table'))
    row_spec = P(('replica', 'table'))
    up = [(i, (i + 1) % data_n) for i in range(data_n)]
    down = [(i, (i + data_n - 1) % data_n) for i in range(data_n)]
    over = [(i, (i + 2) % data_n) for i in range(data_n)]

    def device_step(tok_loc, dy_loc, u_loc, v_loc, wanted_loc, pick_loc, gate_loc):
        n_local, width = u_loc.shape
        toks = tok_loc.shape[0]
        pool = wanted_loc.shape[1] // table_n
        tiles_n = n_local // 8
        pick = pick_loc.transpose(1, 2, 0).reshape(-1, toks)
        gate = gate_loc.transpose(1, 2, 0).reshape(-1, toks)
        ids = share_ids(wanted_loc, table_n, pool)
        rows = fetch(ids, u_loc.reshape(tiles_n, 8, width), v_loc.reshape(tiles_n, 8, width), table_n, pool)
        w_all, c_all, rows_in, own_u, own_v, to_next, prev_v, next_u, to_prev, late, all_ids = exchange(rows, tok_loc, dy_loc, pick, gate, ids, table_n, data_n, pool)
        far = (lax.ppermute(to_next, 'data', up), lax.ppermute(to_prev, 'data', down), lax.ppermute(late, 'data', over))
        near = (own_u, own_v, to_next, prev_v, next_u, to_prev, late)
        zero_u, zero_v, y_loc, dx_loc, sum_u, sum_v, rank, spot, lst = fill(all_ids, w_all, c_all, rows_in, near, tiles_n, pool)
        grad_u, grad_v = write_tiles(lst, rank, spot, far, sum_u, sum_v, zero_u, zero_v, blocks_of(table_n)[1] * pool)
        return y_loc, dx_loc, grad_u.reshape(n_local, width), grad_v.reshape(n_local, width)

    return jax.shard_map(device_step, mesh=mesh, in_specs=(tok_spec, tok_spec, row_spec, row_spec, tok_spec, tok_spec, tok_spec), out_specs=(tok_spec, tok_spec, row_spec, row_spec), check_vma=False)
```

time: 101 us -> 75.8 us (0.75)
  Pallas kernels: 91.8 us -> 71 us
  local copies, waits for them, and re-layouts: 5.73 us -> 0.7 us
    pallas_call x1, Pallas kernels: 44.2 us -> 32.3 us  [exchange(): pl.pallas_call(functools.partial(exchange_kernel, table_n, data_n, pool),...]
    pallas_call x2, Pallas kernels: 16.4 us -> 11.2 us  [the longest x1 7.12 us: share_ids(): pl.pallas_call(functools.partial(ids_kernel, table_n, pool), out_shape=ja...]
    unnamed x12 -> x10, local copies, waits for them, and re-layouts: 5.73 us -> 0.7 us
    pallas_call x1, Pallas kernels: 24.5 us -> 21.9 us  [fill(): pl.pallas_call(functools.partial(fill_kernel, pool, tiles_n * 8), out_sha...]
    pallas_call x1, Pallas kernels: 6.77 us -> 5.58 us  [fetch(): pl.pallas_call(functools.partial(fetch_kernel, table_n, pool, u_tiles.sha...]
    ppermute x2 -> x3, starting transfers between devices: 2.76 us -> 3.45 us  [the longest x1 2.12 us: device_step(): lax.ppermute(to_prev, 'data', down)]
  transfers between devices with their start and end apart: 2 -> 3, of which waited for: 0 -> 0; matrix products, arithmetic and copies ran while one was open for 0% -> 0% of each run, Pallas kernels for 24% -> 29%
where the time goes in v2:
time: 75.8 us; the launch traced here: 75.9 us
  Pallas kernels  71 us (94%)
  starting transfers between devices  3.45 us (5%)
  between operations  0.76 us (1%)
    pallas_call x1, Pallas kernels, exchange(): pl.pallas_call(functools.partial(exchange_kernel, table_n, data_n, pool),...  32.3 us
    pallas_call x1, Pallas kernels, fill(): pl.pallas_call(functools.partial(fill_kernel, pool, tiles_n * 8), out_sha...  21.9 us
    pallas_call x1, Pallas kernels, share_ids(): pl.pallas_call(functools.partial(ids_kernel, table_n, pool), out_shape=ja...  7.12 us
    pallas_call x1, Pallas kernels, fetch(): pl.pallas_call(functools.partial(fetch_kernel, table_n, pool, u_tiles.sha...  5.58 us
    pallas_call x1, Pallas kernels, write_tiles(): pl.pallas_call(functools.partial(tiles_kernel, near), out_shape=(jax.Shap...  4.11 us
    ppermute x1, starting transfers between devices, device_step(): lax.ppermute(to_prev, 'data', down)  2.12 us
  transfers between devices with their start and end apart: 3, of which 0 were waited for; matrix products, arithmetic and copies ran while one was open for 0% of the time, Pallas kernels for 29%

profile of v2, /device:TPU:97, one launch (start us, length us, event | category | flops | bytes accessed | tf_op | source)
XLA Modules:
  0.0 75.9 jit_solution(5688047490247387370)
XLA Ops:
  0.6 0.0 copy-start.4
  0.6 0.7 copy-done.4
  1.3 7.1 %share_ids.1.ids_ref = s32[8,1,128]{2,1,0:T(1,128)S(1)} custom-call(s32[1,256]{1,0:T(1,128)S(1)} %copy-done.4), custom_call_target="tpu_custom_call" | custom-call | tf_op jit(solution)/shard_map/share_ids/pallas_call | solution.py:76
  8.4 0.0 copy-start
  8.4 0.0 copy-start.1
  8.5 0.0 copy-start.2
  8.5 0.0 copy-start.3
  8.5 5.6 %fetch_rows.1.send_ref = bf16[8,2,32,1024]{3,2,1,0:T(8,128)(2,1)S(1)} custom-call(s32[8,1,128]{2,1,0:T(1,128)S(1)} %share_ids.1.ids_ref, bf16[2048,8,1024]{2,1,0:T(8,128)(2,1)} %bitcast.12, bf16[2048,8,1024]{2,1,0:T(8,128)(2,1)} %bitcast.13), custom_call_target="tpu_custom_call" | custom-call | tf_op jit(solution)/shard_map/fetch_rows/pallas_call | solution.py:121
  14.1 0.0 copy-done
  14.1 0.0 copy-done.1
  14.1 0.0 copy-done.2
  14.1 0.0 copy-done.3
  14.1 32.3 %exchange.1 = (f32[256,128]{1,0:T(8,128)S(1)}, f32[256,128]{1,0:T(8,128)S(1)}, bf16[8,2,32,1024]{3,2,1,0:T(8,128)(2,1)S(1)}, bf16[6,32,1024]{2,1,0:T(8,128)(2,1)...) custom-call(bf16[8,2,32,1024]{3,2,1,0:T(8,128)(2,1)S(1)} %fetch_rows, ...), custom_call_target="tpu_custom_call" | custom-call | tf_op jit(solution)/shard_map/exchange/pallas_call | solution.py:259
  46.4 0.6 collective-permute-start
  47.0 2.1 %collective-permute-start.1 = (bf16[10,32,1024]{2,1,0:T(8,128)(2,1)S(1)}, bf16[10,32,1024]{2,1,0:T(8,128)(2,1)S(1)}, u32[]{:S(2)}, u32[]{:S(2)}) collective-permute-start(bf16[10,32,1024]{2,1,0:T(8,128)(2,1)S(1)} %get-tuple-element.35.to_prev), channel_id=1, source_target_pairs={{0,24},{8,0},{16,8},{24,16},{1,25},{9,1},{17,9},{25,17},{2,26},{10... | collective-permute-start | bytes 1966088 | tf_op jit(solution)/shard_map/ppermute | solution.py:532
  49.2 0.7 collective-permute-start.2
  49.8 21.9 %zero_tables.1 = (bf16[2048,8,1024]{2,1,0:T(8,128)(2,1)}, bf16[2048,8,1024]{2,1,0:T(8,128)(2,1)}, bf16[128,1024]{1,0:T(8,128)(2,1)}, bf16[128,1024]{1,0:T(8,128)...) custom-call(s32[4,8,1,128]{3,2,1,0:T(1,128)S(1)} %get-tuple-element., ...), custom_call_target="tpu_custom_call" | custom-call | bytes 67108864 | tf_op jit(solution)/shard_map/zero_tables/pallas_call | solution.py:400
  71.8 0.0 collective-permute-done.2.late_far
  71.8 0.0 collective-permute-done.from_prev
  71.8 0.0 collective-permute-done.1.from_next
  71.8 4.1 %write_tiles.1 = (bf16[2048,8,1024]{2,1,0:T(8,128)(2,1)}, bf16[2048,8,1024]{2,1,0:T(8,128)(2,1)}) custom-call(s32[16,128]{1,0:T(8,128)S(1)} %get-tuple-element.39.list_ref, f32[1,1024]{1,0:T(1,128)S(1)} %get-tuple-element.40.rank_ref, f32[8,128]{1,0:T(8,128)S(1)} %get-tuple-element.41.spot_ref, ...), custom_call_target="tpu_custom_call", output_to_operand_aliasing={{0}: (8, {}), {1}: (9, {})} | custom-call | tf_op jit(solution)/shard_map/write_tiles/pallas_call | solution.py:497
Async XLA Ops:
  0.6 0.7 copy-start.4
  8.4 5.6 %copy-start = (bf16[128,1024]{1,0:T(8,128)(2,1)S(1)}, bf16[128,1024]{1,0:T(8,128)(2,1)}, u32[]{:S(2)}) copy-start(bf16[128,1024]{1,0:T(8,128)(2,1)} %x_ref.1) | copy-start | bytes 786436
  8.4 5.6 %copy-start.1 = (bf16[128,1024]{1,0:T(8,128)(2,1)S(1)}, bf16[128,1024]{1,0:T(8,128)(2,1)}, u32[]{:S(2)}) copy-start(bf16[128,1024]{1,0:T(8,128)(2,1)} %dy_ref.1) | copy-start | bytes 786436
  8.5 5.6 %copy-start.2 = (s32[128,4,32]{0,2,1:T(8,128)S(1)}, s32[128,4,32]{0,2,1:T(8,128)}, u32[]{:S(2)}) copy-start(s32[128,4,32]{0,2,1:T(8,128)} %param.12) | copy-start | bytes 196612
  8.5 5.6 %copy-start.3 = (f32[128,4,32]{0,2,1:T(8,128)S(1)}, f32[128,4,32]{0,2,1:T(8,128)}, u32[]{:S(2)}) copy-start(f32[128,4,32]{0,2,1:T(8,128)} %param.13) | copy-start | bytes 196612
  46.4 25.4 %collective-permute-start = (bf16[10,32,1024]{2,1,0:T(8,128)(2,1)S(1)}, bf16[10,32,1024]{2,1,0:T(8,128)(2,1)S(1)}, u32[]{:S(2)}, u32[]{:S(2)}) collective-permute-start(bf16[10,32,1024]{2,1,0:T(8,128)(2,1)S(1)} %get-tuple-element.32.to_next), channel_id=1, source_target_pairs={{0,8},{8,16},{16,24},{24,0},{1,9},{9,17},{17,25},{25,1},{2,10},{10... | collective-permute-start | bytes 1966088 | tf_op jit(solution)/shard_map/ppermute | solution.py:532
  47.0 24.8 %collective-permute-start.1 = (bf16[10,32,1024]{2,1,0:T(8,128)(2,1)S(1)}, bf16[10,32,1024]{2,1,0:T(8,128)(2,1)S(1)}, u32[]{:S(2)}, u32[]{:S(2)}) collective-permute-start(bf16[10,32,1024]{2,1,0:T(8,128)(2,1)S(1)} %get-tuple-element.35.to_prev), channel_id=1, source_target_pairs={{0,24},{8,0},{16,8},{24,16},{1,25},{9,1},{17,9},{25,17},{2,26},{10... | collective-permute-start | bytes 1966088 | tf_op jit(solution)/shard_map/ppermute | solution.py:532
  49.2 22.6 %collective-permute-start.2 = (bf16[2,2,32,1024]{3,2,1,0:T(8,128)(2,1)S(1)}, bf16[2,2,32,1024]{3,2,1,0:T(8,128)(2,1)S(1)}, u32[]{:S(2)}, u32[]{:S(2)}) collective-permute-start(bf16[2,2,32,1024]{3,2,1,0:T(8,128)(2,1)S(1)} %get-tuple-element.36.late), channel_id=1, source_target_pairs={{0,16},{8,24},{16,0},{24,8},{1,17},{9,25},{17,1},{25,9},{2,18},{10... | collective-permute-start | bytes 786440 | tf_op jit(solution)/shard_map/ppermute | solution.py:532

commit v3 on v2

--- a/solution.py
+++ b/solution.py
@@ -51,7 +51,7 @@
     return lax.dot_general(lhs, rhs, (((1,), (1,)), ((), ())), preferred_element_type=F32)
 
 
-def ids_kernel(table_n, pool, wanted_ref, ids_ref, out_buf, land, send_sem, recv_sem):
+def ids_kernel(table_n, pool, wanted_ref, ids_ref, out_buf, send_sem, recv_sem):
     me = lax.axis_index('table')
     others = range(1, table_n)
     barrier = pltpu.get_barrier_semaphore()
@@ -59,16 +59,15 @@
         pl.semaphore_signal(barrier, inc=1, device_id={'table': partner(me, k)}, device_id_type=MESH)
     for e in range(table_n):
         out_buf[e, :, 0:pool] = wanted_ref[:, e * pool:(e + 1) * pool]
-    land[0] = out_buf[me]
+    ids_ref[0] = out_buf[me]
     pl.semaphore_wait(barrier, table_n - 1)
     copies = []
     for k in others:
         to = partner(me, k)
-        copies.append(pltpu.make_async_remote_copy(src_ref=out_buf.at[to], dst_ref=land.at[k], send_sem=send_sem.at[k], recv_sem=recv_sem.at[k], device_id={'table': to}, device_id_type=MESH))
+        copies.append(pltpu.make_async_remote_copy(src_ref=out_buf.at[to], dst_ref=ids_ref.at[k], send_sem=send_sem.at[k], recv_sem=recv_sem.at[k], device_id={'table': to}, device_id_type=MESH))
         copies[-1].start()
     for one in copies:
         one.wait()
-    ids_ref[...] = land[...]
 
 
 def share_ids(wanted, table_n, pool):
@@ -79,7 +78,6 @@
         in_specs=[vm],
         out_specs=vm,
         scratch_shapes=[
-            pltpu.VMEM((table_n, 1, LANES), jnp.int32),
             pltpu.VMEM((table_n, 1, LANES), jnp.int32),
             pltpu.SemaphoreType.DMA((table_n,)),
             pltpu.SemaphoreType.DMA((table_n,)),
@@ -129,7 +127,7 @@
     )(ids, u_tiles, v_tiles)
 
 
-PLAN = "a1 a2 a6 a3 a7 s0 i0 w1 s1 w2 w6 a4 w3 w7 a5 s2 s6 s3 s7 w4 w5 x4 x5"
+PLAN = "a2 a6 a3 a1 a4 a7 w1 s0 i0 s1 w6 w3 w7 w2 s6 a5 s3 s7 s2 w4 w5 x4 x5"
 
 
 def plan_of(order, early):
@@ -287,6 +285,10 @@
     return jnp.concatenate([jnp.broadcast_to(row[:, c * 128:(c + 1) * 128], (128, 128)).T for c in range(n // 128)], axis=0)
 
 
+FILL = 128
+REST = 3
+
+
 def fill_kernel(pool, n_local, ids_ref, w_ref, c_ref, rows_ref, own_u, own_v, to_next, prev_v, next_u, to_prev, late,
                 du_ref, dv_ref, y_ref, dx_ref, sum_u, sum_v, rank_ref, spot_ref, list_ref,
                 zero, zsem):
@@ -297,8 +299,11 @@
     zero[...] = jnp.zeros_like(zero)
 
     def start(i, carry):
-        for w, ref in enumerate((du_ref, dv_ref)):
-            pltpu.make_async_copy(zero, ref.at[pl.ds(i * step, step)], zsem.at[w]).start()
+        pltpu.make_async_copy(zero, du_ref.at[pl.ds(i * step, step)], zsem.at[0]).start()
+
+        @pl.when(i < tiles_n // step - REST)
+        def _():
+            pltpu.make_async_copy(zero, dv_ref.at[pl.ds(i * step, step)], zsem.at[1]).start()
         return carry
     lax.fori_loop(0, tiles_n // step, start, 0)
 
@@ -384,8 +389,9 @@
             out[span, :] = jnp.dot(hot, stack([own[...], late[w], prev[0:own.shape[0]], nxt[0:own.shape[0]]]), preferred_element_type=F32)
         return carry
     lax.fori_loop(0, n_chunks, add_up, 0)
-    for w, ref in enumerate((du_ref, dv_ref)):
-        pltpu.make_async_copy(ref, ref, zsem.at[w]).wait()
+    filled = dv_ref.at[pl.ds(0, tiles_n - REST * step)]
+    pltpu.make_async_copy(du_ref, du_ref, zsem.at[0]).wait()
+    pltpu.make_async_copy(filled, filled, zsem.at[1]).wait()
 
 
 def fill(ids, w_all, c_all, rows, near, tiles_n, pool):
@@ -395,7 +401,7 @@
     width = rows.shape[3]
     vm = pl.BlockSpec(memory_space=pltpu.VMEM)
     hbm = pl.BlockSpec(memory_space=pl.ANY)
-    step = 128
+    step = FILL
     tok_shape = jax.ShapeDtypeStruct((toks, width), BF16)
     return pl.pallas_call(
         functools.partial(fill_kernel, pool, tiles_n * 8),
@@ -414,13 +420,23 @@
     )(ids, w_all, c_all, rows, *near)
 
 
-def tiles_kernel(near, list_ref, rank_ref, spot_ref, from_prev, from_next, late_far, sum_u, sum_v, zero_u, zero_v, du_ref, dv_ref, done, stage, wsem):
+def tiles_kernel(near, list_ref, rank_ref, spot_ref, from_prev, from_next, late_far, sum_u, sum_v, zero_u, zero_v, du_ref, dv_ref, done, stage, zero, wsem, zsem):
     n = rank_ref.shape[1]
     width = du_ref.shape[2]
     lines = n // LANES
     n_tiles = list_ref[lines, 0]
     n_rows = list_ref[lines, 1]
     n_chunks = lax.div(n_rows + (LANES - 1), LANES)
+    step = zero.shape[0]
+    left = FILL * REST
+    kept = du_ref.shape[0] - left
+    zero[...] = jnp.zeros_like(zero)
+
+    def start(i, carry):
+        pltpu.make_async_copy(zero, dv_ref.at[pl.ds(kept + i * step, step)], zsem).start()
+        return carry
+    lax.fori_loop(0, left // step, start, 0)
+
     target = lax.broadcasted_iota(jnp.int32, (LANES, n - near), 0).astype(F32)
 
     def finish(c, carry):
@@ -447,10 +463,6 @@
 
     def build(c, carry):
         slot = lax.rem(c, ring)
-
-        @pl.when(c >= ring)
-        def _():
-            drain(slot)
         start = lax.div(list_ref[lines + 1, c], LANES)
         end = lax.div(list_ref[lines + 1, c + 1] + (LANES - 1), LANES)
 
@@ -466,15 +478,47 @@
                 stage[slot, w] = stage[slot, w] + val
             return inner
         lax.fori_loop(start + 1, end, more, 0)
-
-        def put(q, inner):
-            tile = list_ref[lax.div(q, LANES), lax.rem(q, LANES)]
-            pltpu.make_async_copy(stage.at[slot, 0, q - c * per], du_ref.at[tile], wsem.at[slot]).start()
-            pltpu.make_async_copy(stage.at[slot, 1, q - c * per], dv_ref.at[tile], wsem.at[slot]).start()
-            return inner
-        lax.fori_loop(c * per, jnp.minimum(n_tiles, (c + 1) * per), put, 0)
-        return carry
-    lax.fori_loop(0, n_builds, build, 0)
+        return carry
+
+    def put(c, w, ref):
+        slot = lax.rem(c, ring)
+        line = lax.div(c * per, LANES)
+        base = lax.rem(c * per, LANES)
+        count = n_tiles - c * per
+
+        def one(i, carry):
+            pltpu.make_async_copy(stage.at[slot, w, i], ref.at[list_ref[line, base + i]], wsem.at[slot]).start()
+            return carry
+
+        @pl.when(count >= per)
+        def _():
+            for i in range(per):
+                one(i, 0)
+
+        @pl.when(count < per)
+        def _():
+            lax.fori_loop(0, count, one, 0)
+
+    def first(c, carry):
+        build(c, 0)
+        put(c, 0, du_ref)
+        return carry
+    lax.fori_loop(0, jnp.minimum(n_builds, ring), first, 0)
+    tail = dv_ref.at[pl.ds(kept, left)]
+    pltpu.make_async_copy(tail, tail, zsem).wait()
+
+    def second(c, carry):
+        put(c, 1, dv_ref)
+        return carry
+    lax.fori_loop(0, jnp.minimum(n_builds, ring), second, 0)
+
+    def later(c, carry):
+        drain(lax.rem(c, ring))
+        build(c, 0)
+        put(c, 0, du_ref)
+        put(c, 1, dv_ref)
+        return carry
+    lax.fori_loop(ring, n_builds, later, 0)
 
     def full(c, carry):
         drain(lax.rem(c, ring))
@@ -502,7 +546,9 @@
         scratch_shapes=[
             pltpu.VMEM((2, n, width), BF16),
             pltpu.VMEM((8, 2, 32, 8, width), BF16),
+            pltpu.VMEM((FILL // 2, 8, width), BF16),
             pltpu.SemaphoreType.DMA((8,)),
+            pltpu.SemaphoreType.DMA,
         ],
         input_output_aliases={8: 0, 9: 1},
         compiler_params=pltpu.CompilerParams(vmem_limit_bytes=24 * MIB),

time: 75.8 us -> 74 us (0.976)
  Pallas kernels: 71 us -> 69.3 us
    pallas_call x1, Pallas kernels: 21.9 us -> 20 us  [fill(): pl.pallas_call(functools.partial(fill_kernel, pool, tiles_n * 8), out_sha...]
  transfers between devices with their start and end apart: 3 -> 3, of which waited for: 0 -> 0; matrix products, arithmetic and copies ran while one was open for 0% -> 0% of each run, Pallas kernels for 29% -> 27%
where the time goes in v3:
time: 74 us
  Pallas kernels  69.3 us (94%)
  starting transfers between devices  3.18 us (4%)
  between operations  0.76 us (1%)
    pallas_call x1, Pallas kernels, exchange(): pl.pallas_call(functools.partial(exchange_kernel, table_n, data_n, pool),...  32.5 us
    pallas_call x1, Pallas kernels, fill(): pl.pallas_call(functools.partial(fill_kernel, pool, tiles_n * 8), out_sha...  20 us
    pallas_call x1, Pallas kernels, share_ids(): pl.pallas_call(functools.partial(ids_kernel, table_n, pool), out_shape=ja...  7.12 us
    pallas_call x1, Pallas kernels, fetch(): pl.pallas_call(functools.partial(fetch_kernel, table_n, pool, u_tiles.sha...  5.2 us
    pallas_call x1, Pallas kernels, write_tiles(): pl.pallas_call(functools.partial(tiles_kernel, near), out_shape=(jax.Shap...  4.53 us
    ppermute x1, starting transfers between devices, device_step(): lax.ppermute(to_prev, 'data', down)  2.24 us
  transfers between devices with their start and end apart: 3, of which 0 were waited for; matrix products, arithmetic and copies ran while one was open for 0% of the time, Pallas kernels for 27%

profile of v3, /device:TPU:97, one launch (start us, length us, event | category | flops | bytes accessed | tf_op | source)
XLA Modules:
  0.0 74.0 jit_solution(16240670920356792760)
XLA Ops:
  0.6 0.0 copy-start.4
  0.6 0.7 copy-done.4
  1.3 7.1 %share_ids.1.ids_ref = s32[8,1,128]{2,1,0:T(1,128)S(1)} custom-call(s32[1,256]{1,0:T(1,128)S(1)} %copy-done.4), custom_call_target="tpu_custom_call" | custom-call | tf_op jit(solution)/shard_map/share_ids/pallas_call | solution.py:75
  8.4 0.0 copy-start
  8.4 0.0 copy-start.1
  8.5 0.0 copy-start.2
  8.5 0.0 copy-start.3
  8.5 5.2 %fetch_rows.1.send_ref = bf16[8,2,32,1024]{3,2,1,0:T(8,128)(2,1)S(1)} custom-call(s32[8,1,128]{2,1,0:T(1,128)S(1)} %share_ids.1.ids_ref, bf16[2048,8,1024]{2,1,0:T(8,128)(2,1)} %bitcast.12, bf16[2048,8,1024]{2,1,0:T(8,128)(2,1)} %bitcast.13), custom_call_target="tpu_custom_call" | custom-call | tf_op jit(solution)/shard_map/fetch_rows/pallas_call | solution.py:119
  13.7 0.0 copy-done
  13.7 0.0 copy-done.1
  13.7 0.0 copy-done.2
  13.7 0.0 copy-done.3
  13.7 32.5 %exchange.1 = (f32[256,128]{1,0:T(8,128)S(1)}, f32[256,128]{1,0:T(8,128)S(1)}, bf16[8,2,32,1024]{3,2,1,0:T(8,128)(2,1)S(1)}, bf16[6,32,1024]{2,1,0:T(8,128)(2,1)...) custom-call(bf16[8,2,32,1024]{3,2,1,0:T(8,128)(2,1)S(1)} %fetch_rows, ...), custom_call_target="tpu_custom_call" | custom-call | tf_op jit(solution)/shard_map/exchange/pallas_call | solution.py:257
  46.2 0.5 collective-permute-start
  46.7 2.2 %collective-permute-start.1 = (bf16[10,32,1024]{2,1,0:T(8,128)(2,1)S(1)}, bf16[10,32,1024]{2,1,0:T(8,128)(2,1)S(1)}, u32[]{:S(2)}, u32[]{:S(2)}) collective-permute-start(bf16[10,32,1024]{2,1,0:T(8,128)(2,1)S(1)} %get-tuple-element.35.to_prev), channel_id=1, source_target_pairs={{0,24},{8,0},{16,8},{24,16},{1,25},{9,1},{17,9},{25,17},{2,26},{10... | collective-permute-start | bytes 1966088 | tf_op jit(solution)/shard_map/ppermute | solution.py:578
  49.0 0.4 collective-permute-start.2
  49.4 20.0 %zero_tables.1 = (bf16[2048,8,1024]{2,1,0:T(8,128)(2,1)}, bf16[2048,8,1024]{2,1,0:T(8,128)(2,1)}, bf16[128,1024]{1,0:T(8,128)(2,1)}, bf16[128,1024]{1,0:T(8,128)...) custom-call(s32[4,8,1,128]{3,2,1,0:T(1,128)S(1)} %get-tuple-element., ...), custom_call_target="tpu_custom_call" | custom-call | bytes 67108864 | tf_op jit(solution)/shard_map/zero_tables/pallas_call | solution.py:406
  69.4 0.0 collective-permute-done.2.late_far
  69.4 0.0 collective-permute-done.from_prev
  69.4 0.0 collective-permute-done.1.from_next
  69.4 4.5 %write_tiles.1 = (bf16[2048,8,1024]{2,1,0:T(8,128)(2,1)}, bf16[2048,8,1024]{2,1,0:T(8,128)(2,1)}) custom-call(s32[16,128]{1,0:T(8,128)S(1)} %get-tuple-element.39.list_ref, f32[1,1024]{1,0:T(1,128)S(1)} %get-tuple-element.40.rank_ref, f32[8,128]{1,0:T(8,128)S(1)} %get-tuple-element.41.spot_ref, ...), custom_call_target="tpu_custom_call", output_to_operand_aliasing={{0}: (8, {}), {1}: (9, {})} | custom-call | tf_op jit(solution)/shard_map/write_tiles/pallas_call | solution.py:541
Async XLA Ops:
  0.6 0.7 copy-start.4
  8.4 5.3 %copy-start = (bf16[128,1024]{1,0:T(8,128)(2,1)S(1)}, bf16[128,1024]{1,0:T(8,128)(2,1)}, u32[]{:S(2)}) copy-start(bf16[128,1024]{1,0:T(8,128)(2,1)} %x_ref.1) | copy-start | bytes 786436
  8.4 5.3 %copy-start.1 = (bf16[128,1024]{1,0:T(8,128)(2,1)S(1)}, bf16[128,1024]{1,0:T(8,128)(2,1)}, u32[]{:S(2)}) copy-start(bf16[128,1024]{1,0:T(8,128)(2,1)} %dy_ref.1) | copy-start | bytes 786436
  8.5 5.3 %copy-start.2 = (s32[128,4,32]{0,2,1:T(8,128)S(1)}, s32[128,4,32]{0,2,1:T(8,128)}, u32[]{:S(2)}) copy-start(s32[128,4,32]{0,2,1:T(8,128)} %param.12) | copy-start | bytes 196612
  8.5 5.2 %copy-start.3 = (f32[128,4,32]{0,2,1:T(8,128)S(1)}, f32[128,4,32]{0,2,1:T(8,128)}, u32[]{:S(2)}) copy-start(f32[128,4,32]{0,2,1:T(8,128)} %param.13) | copy-start | bytes 196612
  46.2 23.2 %collective-permute-start = (bf16[10,32,1024]{2,1,0:T(8,128)(2,1)S(1)}, bf16[10,32,1024]{2,1,0:T(8,128)(2,1)S(1)}, u32[]{:S(2)}, u32[]{:S(2)}) collective-permute-start(bf16[10,32,1024]{2,1,0:T(8,128)(2,1)S(1)} %get-tuple-element.32.to_next), channel_id=1, source_target_pairs={{0,8},{8,16},{16,24},{24,0},{1,9},{9,17},{17,25},{25,1},{2,10},{10... | collective-permute-start | bytes 1966088 | tf_op jit(solution)/shard_map/ppermute | solution.py:578
  46.7 22.7 %collective-permute-start.1 = (bf16[10,32,1024]{2,1,0:T(8,128)(2,1)S(1)}, bf16[10,32,1024]{2,1,0:T(8,128)(2,1)S(1)}, u32[]{:S(2)}, u32[]{:S(2)}) collective-permute-start(bf16[10,32,1024]{2,1,0:T(8,128)(2,1)S(1)} %get-tuple-element.35.to_prev), channel_id=1, source_target_pairs={{0,24},{8,0},{16,8},{24,16},{1,25},{9,1},{17,9},{25,17},{2,26},{10... | collective-permute-start | bytes 1966088 | tf_op jit(solution)/shard_map/ppermute | solution.py:578
  49.0 20.5 %collective-permute-start.2 = (bf16[2,2,32,1024]{3,2,1,0:T(8,128)(2,1)S(1)}, bf16[2,2,32,1024]{3,2,1,0:T(8,128)(2,1)S(1)}, u32[]{:S(2)}, u32[]{:S(2)}) collective-permute-start(bf16[2,2,32,1024]{3,2,1,0:T(8,128)(2,1)S(1)} %get-tuple-element.36.late), channel_id=1, source_target_pairs={{0,16},{8,24},{16,0},{24,8},{1,17},{9,25},{17,1},{25,9},{2,18},{10... | collective-permute-start | bytes 786440 | tf_op jit(solution)/shard_map/ppermute | solution.py:578

commit v4 on v3

--- a/solution.py
+++ b/solution.py
@@ -108,9 +108,10 @@
                     line = jnp.bitwise_and(ids_ref[k, 0, s] - first, 7)
                     turned = pltpu.roll(tiles[k, which, s].astype(F32), jnp.bitwise_and(i - line + 8, 7), 0)
                     out = jnp.where(sub == i, turned, out)
-                rows_ref[k, which, pl.ds(pl.multiple_of(g * 8, 8), 8), :] = out.astype(BF16)
+                rows_ref[k, which, g * 8:(g + 1) * 8, :] = out.astype(BF16)
             return carry
-        lax.fori_loop(0, pool // 8, pull, 0)
+        for g in range(pool // 8):
+            pull(g, 0)
 
 
 def fetch(ids, u_tiles, v_tiles, table_n, pool):
@@ -127,7 +128,7 @@
     )(ids, u_tiles, v_tiles)
 
 
-PLAN = "a2 a6 a3 a1 a4 a7 w1 s0 i0 s1 w6 w3 w7 w2 s6 a5 s3 s7 s2 w4 w5 x4 x5"
+PLAN = "a2 a6 a3 a7 a1 a4 s0 w1 s1 w6 w2 i0 w3 w7 s6 s2 a5 s3 s7 w4 w5 x4 x5"
 
 
 def plan_of(order, early):

time: 74 us -> 73.7 us (level)
  no operation moved by 1% of the time
where the time goes in v4:
time: 73.7 us; the launch traced here: 73.6 us
  Pallas kernels  69.2 us (94%)
  starting transfers between devices  2.9 us (4%)
  between operations  0.77 us (1%)
    pallas_call x1, Pallas kernels, exchange(): pl.pallas_call(functools.partial(exchange_kernel, table_n, data_n, pool),...  32.4 us
    pallas_call x1, Pallas kernels, fill(): pl.pallas_call(functools.partial(fill_kernel, pool, tiles_n * 8), out_sha...  20 us
    pallas_call x1, Pallas kernels, share_ids(): pl.pallas_call(functools.partial(ids_kernel, table_n, pool), out_shape=ja...  7.12 us
    pallas_call x1, Pallas kernels, fetch(): pl.pallas_call(functools.partial(fetch_kernel, table_n, pool, u_tiles.sha...  5.08 us
    pallas_call x1, Pallas kernels, write_tiles(): pl.pallas_call(functools.partial(tiles_kernel, near), out_shape=(jax.Shap...  4.57 us
    ppermute x1, starting transfers between devices, device_step(): lax.ppermute(to_prev, 'data', down)  2.65 us
  transfers between devices with their start and end apart: 3, of which 0 were waited for; matrix products, arithmetic and copies ran while one was open for 0% of the time, Pallas kernels for 27%

profile of v4, /device:TPU:97, one launch (start us, length us, event | category | flops | bytes accessed | tf_op | source)
XLA Modules:
  0.0 73.6 jit_solution(9019855781900202638)
XLA Ops:
  0.6 0.0 copy-start.4
  0.6 0.7 copy-done.4
  1.3 7.1 %share_ids.1.ids_ref = s32[8,1,128]{2,1,0:T(1,128)S(1)} custom-call(s32[1,256]{1,0:T(1,128)S(1)} %copy-done.4), custom_call_target="tpu_custom_call" | custom-call | tf_op jit(solution)/shard_map/share_ids/pallas_call | solution.py:75
  8.4 0.0 copy-start
  8.4 0.0 copy-start.1
  8.5 0.0 copy-start.2
  8.5 0.0 copy-start.3
  8.5 5.1 %fetch_rows.1.send_ref = bf16[8,2,32,1024]{3,2,1,0:T(8,128)(2,1)S(1)} custom-call(s32[8,1,128]{2,1,0:T(1,128)S(1)} %share_ids.1.ids_ref, bf16[2048,8,1024]{2,1,0:T(8,128)(2,1)} %bitcast.12, bf16[2048,8,1024]{2,1,0:T(8,128)(2,1)} %bitcast.13), custom_call_target="tpu_custom_call" | custom-call | tf_op jit(solution)/shard_map/fetch_rows/pallas_call | solution.py:120
  13.6 0.0 copy-done
  13.6 0.0 copy-done.1
  13.6 0.0 copy-done.2
  13.6 0.0 copy-done.3
  13.6 32.4 %exchange.1 = (f32[256,128]{1,0:T(8,128)S(1)}, f32[256,128]{1,0:T(8,128)S(1)}, bf16[8,2,32,1024]{3,2,1,0:T(8,128)(2,1)S(1)}, bf16[6,32,1024]{2,1,0:T(8,128)(2,1)...) custom-call(bf16[8,2,32,1024]{3,2,1,0:T(8,128)(2,1)S(1)} %fetch_rows, ...), custom_call_target="tpu_custom_call" | custom-call | tf_op jit(solution)/shard_map/exchange/pallas_call | solution.py:258
  46.0 0.1 collective-permute-start
  46.1 2.6 %collective-permute-start.1 = (bf16[10,32,1024]{2,1,0:T(8,128)(2,1)S(1)}, bf16[10,32,1024]{2,1,0:T(8,128)(2,1)S(1)}, u32[]{:S(2)}, u32[]{:S(2)}) collective-permute-start(bf16[10,32,1024]{2,1,0:T(8,128)(2,1)S(1)} %get-tuple-element.35.to_prev), channel_id=1, source_target_pairs={{0,24},{8,0},{16,8},{24,16},{1,25},{9,1},{17,9},{25,17},{2,26},{10... | collective-permute-start | bytes 1966088 | tf_op jit(solution)/shard_map/ppermute | solution.py:579
  48.8 0.1 collective-permute-start.2
  48.9 20.0 %zero_tables.1 = (bf16[2048,8,1024]{2,1,0:T(8,128)(2,1)}, bf16[2048,8,1024]{2,1,0:T(8,128)(2,1)}, bf16[128,1024]{1,0:T(8,128)(2,1)}, bf16[128,1024]{1,0:T(8,128)...) custom-call(s32[4,8,1,128]{3,2,1,0:T(1,128)S(1)} %get-tuple-element., ...), custom_call_target="tpu_custom_call" | custom-call | bytes 67108864 | tf_op jit(solution)/shard_map/zero_tables/pallas_call | solution.py:407
  69.0 0.0 collective-permute-done.2.late_far
  69.0 0.0 collective-permute-done.from_prev
  69.0 0.0 collective-permute-done.1.from_next
  69.0 4.6 %write_tiles.1 = (bf16[2048,8,1024]{2,1,0:T(8,128)(2,1)}, bf16[2048,8,1024]{2,1,0:T(8,128)(2,1)}) custom-call(s32[16,128]{1,0:T(8,128)S(1)} %get-tuple-element.39.list_ref, f32[1,1024]{1,0:T(1,128)S(1)} %get-tuple-element.40.rank_ref, f32[8,128]{1,0:T(8,128)S(1)} %get-tuple-element.41.spot_ref, ...), custom_call_target="tpu_custom_call", output_to_operand_aliasing={{0}: (8, {}), {1}: (9, {})} | custom-call | tf_op jit(solution)/shard_map/write_tiles/pallas_call | solution.py:542
Async XLA Ops:
  0.6 0.7 copy-start.4
  8.4 5.1 %copy-start = (bf16[128,1024]{1,0:T(8,128)(2,1)S(1)}, bf16[128,1024]{1,0:T(8,128)(2,1)}, u32[]{:S(2)}) copy-start(bf16[128,1024]{1,0:T(8,128)(2,1)} %x_ref.1) | copy-start | bytes 786436
  8.4 5.1 %copy-start.1 = (bf16[128,1024]{1,0:T(8,128)(2,1)S(1)}, bf16[128,1024]{1,0:T(8,128)(2,1)}, u32[]{:S(2)}) copy-start(bf16[128,1024]{1,0:T(8,128)(2,1)} %dy_ref.1) | copy-start | bytes 786436
  8.5 5.1 %copy-start.2 = (s32[128,4,32]{0,2,1:T(8,128)S(1)}, s32[128,4,32]{0,2,1:T(8,128)}, u32[]{:S(2)}) copy-start(s32[128,4,32]{0,2,1:T(8,128)} %param.12) | copy-start | bytes 196612
  8.5 5.1 %copy-start.3 = (f32[128,4,32]{0,2,1:T(8,128)S(1)}, f32[128,4,32]{0,2,1:T(8,128)}, u32[]{:S(2)}) copy-start(f32[128,4,32]{0,2,1:T(8,128)} %param.13) | copy-start | bytes 196612
  46.0 23.0 %collective-permute-start = (bf16[10,32,1024]{2,1,0:T(8,128)(2,1)S(1)}, bf16[10,32,1024]{2,1,0:T(8,128)(2,1)S(1)}, u32[]{:S(2)}, u32[]{:S(2)}) collective-permute-start(bf16[10,32,1024]{2,1,0:T(8,128)(2,1)S(1)} %get-tuple-element.32.to_next), channel_id=1, source_target_pairs={{0,8},{8,16},{16,24},{24,0},{1,9},{9,17},{17,25},{25,1},{2,10},{10... | collective-permute-start | bytes 1966088 | tf_op jit(solution)/shard_map/ppermute | solution.py:579
  46.1 22.9 %collective-permute-start.1 = (bf16[10,32,1024]{2,1,0:T(8,128)(2,1)S(1)}, bf16[10,32,1024]{2,1,0:T(8,128)(2,1)S(1)}, u32[]{:S(2)}, u32[]{:S(2)}) collective-permute-start(bf16[10,32,1024]{2,1,0:T(8,128)(2,1)S(1)} %get-tuple-element.35.to_prev), channel_id=1, source_target_pairs={{0,24},{8,0},{16,8},{24,16},{1,25},{9,1},{17,9},{25,17},{2,26},{10... | collective-permute-start | bytes 1966088 | tf_op jit(solution)/shard_map/ppermute | solution.py:579
  48.8 20.2 %collective-permute-start.2 = (bf16[2,2,32,1024]{3,2,1,0:T(8,128)(2,1)S(1)}, bf16[2,2,32,1024]{3,2,1,0:T(8,128)(2,1)S(1)}, u32[]{:S(2)}, u32[]{:S(2)}) collective-permute-start(bf16[2,2,32,1024]{3,2,1,0:T(8,128)(2,1)S(1)} %get-tuple-element.36.late), channel_id=1, source_target_pairs={{0,16},{8,24},{16,0},{24,8},{1,17},{9,25},{17,1},{25,9},{2,18},{10... | collective-permute-start | bytes 786440 | tf_op jit(solution)/shard_map/ppermute | solution.py:579
